TPU v7x, 64 devices: a 2x2x8 block of a 4x4x8 slice. The times are simulated.
64 devices in a mesh: dp: 4 (over x, y), ep: 16 (over z, core).
Axes of the slice: x: 2, y: 2, z: 8, core: 2. Of those that a mesh axis runs over, the one named last changes fastest.
The devices are a block of a 4x4x8 slice.
Arguments:
- x_a: bfloat16 [16384, 2048], P(('dp', 'ep')), parts along dimension 0
- route_a: int32 [16384, 8], P(('dp', 'ep')), parts along dimension 0
- gate_a: float32 [16384, 8], P(('dp', 'ep')), parts along dimension 0
- h_b: bfloat16 [16384, 2048], P(('dp', 'ep')), parts along dimension 0
- attn_b: bfloat16 [16384, 2048], P(('dp', 'ep')), parts along dimension 0
- route_b: int32 [16384, 8], P(('dp', 'ep')), parts along dimension 0
- gate_b: float32 [16384, 8], P(('dp', 'ep')), parts along dimension 0
- w_qkv: bfloat16 [2048, 6144], replicated
- w_o: bfloat16 [2048, 2048], replicated
- w_gate: bfloat16 [64, 2048, 1024], P('ep')
- w_up: bfloat16 [64, 2048, 1024], P('ep')
- w_down: bfloat16 [64, 1024, 2048], P('ep')
Outputs:
- output 1: bfloat16 [16384, 2048], P(('dp', 'ep')), parts along dimension 0
- output 2: bfloat16 [16384, 2048], P(('dp', 'ep')), parts along dimension 0
- output 3: bfloat16 [16384, 6144], P(('dp', 'ep')), parts along dimension 0
There are 4 independent parts. A program takes and returns all parts, laid end to end along the dimension named above; an argument that names none is the same for every part.
All inputs are finite; a program needn't handle non-finite values.
Results may differ from a plain program's by a relative error of at most 0.0107879.
Values are sent between devices in bfloat16 or wider.
A program may use at most 768 MiB of HBM per device.

v0:
```python
import jax
import jax.numpy as jnp
from jax import lax
from jax.sharding import PartitionSpec as P


def route_slots(route_ids, n_experts, n_devs, capacity):
    tok_n, top_k = route_ids.shape
    local_n = n_experts // n_devs
    flat_route = route_ids.reshape(tok_n * top_k)
    one_hot = (flat_route[:, None] == jnp.arange(n_experts)[None, :]).astype(jnp.int32)
    slot_rank = jnp.sum((jnp.cumsum(one_hot, axis=0) - 1) * one_hot, axis=1)
    owner = flat_route // local_n
    local_id = flat_route % local_n
    slot_ids = local_id * (n_devs * capacity) + owner * capacity + slot_rank
    return slot_ids.reshape(tok_n, top_k)


def expert_ffn(rows_in, w_gate, w_up, w_down):
    gate_act = jnp.einsum('erd,edf->erf', rows_in, w_gate, preferred_element_type=jnp.float32)
    up_act = jnp.einsum('erd,edf->erf', rows_in, w_up, preferred_element_type=jnp.float32)
    hidden = (jax.nn.silu(gate_act) * up_act).astype(jnp.bfloat16)
    return jnp.einsum('erf,efd->erd', hidden, w_down, preferred_element_type=jnp.float32).astype(jnp.bfloat16)


def moe_local(tokens, route_ids, gate_vals, w_gate, w_up, w_down, n_devs):
    tok_n, model_dim = tokens.shape
    top_k = route_ids.shape[1]
    local_n = w_gate.shape[0]
    n_experts = local_n * n_devs
    capacity = min(tok_n, 2 * ((tok_n * top_k + n_experts - 1) // n_experts))
    n_slots = n_experts * capacity
    slot_ids = route_slots(route_ids, n_experts, n_devs, capacity)
    picker = (slot_ids[:, :, None] == jnp.arange(n_slots)[None, None, :]).astype(jnp.bfloat16)
    placer = jnp.sum(picker, axis=1)
    send_buf = jnp.einsum('ts,td->sd', placer, tokens, preferred_element_type=jnp.float32).astype(jnp.bfloat16)
    send_buf = send_buf.reshape(local_n, n_devs, capacity, model_dim)
    recv_buf = lax.all_to_all(send_buf, 'ep', 1, 1, tiled=True)
    expert_out = expert_ffn(recv_buf.reshape(local_n, n_devs * capacity, model_dim), w_gate, w_up, w_down)
    back_buf = lax.all_to_all(expert_out.reshape(local_n, n_devs, capacity, model_dim), 'ep', 1, 1, tiled=True)
    picked = jnp.einsum('tjs,sd->tjd', picker, back_buf.reshape(n_slots, model_dim), preferred_element_type=jnp.float32)
    mixture = jnp.zeros((tok_n, model_dim), jnp.float32)
    for choice in range(top_k):
        mixture = mixture + gate_vals[:, choice:choice + 1] * picked[:, choice]
    return (tokens.astype(jnp.float32) + mixture).astype(jnp.bfloat16)


def solution(mesh):
    n_devs = mesh.shape['ep']

    def local_step(x_a, route_a, gate_a, h_b, attn_b, route_b, gate_b, w_qkv, w_o, w_gate, w_up, w_down):
        out_a = moe_local(x_a, route_a, gate_a, w_gate, w_up, w_down, n_devs)
        qkv_b = jnp.dot(h_b, w_qkv, preferred_element_type=jnp.float32).astype(jnp.bfloat16)
        proj_b = jnp.dot(attn_b, w_o, preferred_element_type=jnp.float32).astype(jnp.bfloat16)
        mid_b = (h_b.astype(jnp.float32) + proj_b.astype(jnp.float32)).astype(jnp.bfloat16)
        out_b = moe_local(mid_b, route_b, gate_b, w_gate, w_up, w_down, n_devs)
        return out_a, out_b, qkv_b

    row_spec = P(('dp', 'ep'), None)
    full_spec = P(None, None)
    expert_spec = P('ep', None, None)
    return jax.shard_map(
        local_step,
        mesh=mesh,
        in_specs=(row_spec, row_spec, row_spec, row_spec, row_spec, row_spec, row_spec, full_spec, full_spec, expert_spec, expert_spec, expert_spec),
        out_specs=(row_spec, row_spec, row_spec),
        check_vma=False,
    )
```

profile of v0, /device:TPU:21, one launch (start us, length us, event | category | flops | bytes accessed | tf_op | source)
XLA Modules:
  0.0 1676.7 jit_solution(2157871341680214247)
XLA Ops:
  0.6 0.0 copy-start
  0.6 0.9 copy.68
  1.6 0.1 eq.94
  1.7 0.1 eq.90
  1.8 18.1 %reduce-window.16 = s32[64,16,128]{2,1,0:T(8,128)S(1)} reduce-window(s32[64,16,128]{2,1,0:T(8,128)S(1)} %fusion.50, s32[]{:T(128)} %constant.52.clone.1), window={size=1x1x128 pad=0_0x0_0x127_0}, to_apply=%region_4.5 | reduce-window | flops 16646144 | bytes 1048580 | tf_op jit(solution)/shard_map/reduce-window.2
  20.0 0.2 slice.154
  20.2 0.4 copy.78
  20.6 0.2 reduce-window.19
  20.8 0.2 add_add_fusion
  21.0 0.2 fusion.46
  21.2 0.1 reduce_sum.50
  21.3 0.1 copy.72
  21.4 0.7 fusion.57
  22.1 0.6 copy-done.7
  22.7 4.8 fusion.5
  27.5 0.0 copy-done
  27.5 6.9 fusion.10
  34.5 9.3 convolution_convert_fusion
  43.8 14.1 copy.73
  57.9 11.4 all-to-all-start.2
  69.3 0.0 copy-done.11
  69.3 0.1 copy.59
  69.4 0.1 eq.83
  69.5 0.1 eq.79
  69.7 18.1 %reduce-window.14 = s32[64,16,128]{2,1,0:T(8,128)S(1)} reduce-window(s32[64,16,128]{2,1,0:T(8,128)S(1)} %fusion.49, s32[]{:T(128)} %constant.52.clone.1), window={size=1x1x128 pad=0_0x0_0x127_0}, to_apply=%region_0.0 | reduce-window | flops 16646144 | bytes 1048580 | tf_op jit(solution)/shard_map/reduce-window
  87.8 0.2 slice.144
  88.0 0.4 copy.77
  88.5 0.2 reduce-window.15
  88.7 0.2 add_add_fusion.1
  88.9 0.2 fusion.48
  89.1 0.1 reduce_sum.47
  89.2 0.1 copy.63
  89.3 0.0 copy-start.9
  89.3 4.8 fusion.4
  94.1 9.3 convolution_convert_fusion.1
  103.5 14.1 copy.64
  117.6 331.1 %all-to-all-done.2 = bf16[4,16,64,2048]{3,2,0,1:T(8,128)(2,1)} async-done(((bf16[4,16,64,2048]{3,2,0,1:T(8,128)(2,1)}), bf16[4,16,64,2048]{3,2,0,1:T(8,128)(2,1)}, u32[]{:S(2)}, u32[]{:S(2)}) %all-to-all-start.2) | async-done | bytes 16777248 | tf_op jit(solution)/shard_map/all_to_all | solution.py:38
  448.6 7.2 all-to-all-start
  455.8 8.1 copy.74
  464.0 5.7 copy-done.3
  469.7 22.2 %fusion.70 = f32[4,1024,1024]{2,1,0:T(8,128)} fusion(bf16[4,1024,2048]{2,1,0:T(8,128)(2,1)S(1)} %bitcast.212, bf16[4,2048,1024]{2,1,0:T(8,128)(2,1)} %param.21), kind=kOutput, calls=%fused_computation.116 | convolution fusion | flops 17179869184 | bytes 50331648 | tf_op jit(solution)/shard_map/erd,edf->erf/dot_general | solution.py:20
  491.8 29.8 %multiply_convert_fusion = bf16[4,1024,1024]{2,1,0:T(8,128)(2,1)} fusion(f32[4,1024,1024]{2,1,0:T(8,128)} %fusion.70, bf16[4,1024,2048]{2,1,0:T(8,128)(2,1)} %bitcast.213, bf16[4,2048,1024]{2,1,0:T(8,128)(2,1)} %param.22), kind=kOutput, calls=%fused_computation.8 | convolution fusion | flops 17205035008 | bytes 58720256 | tf_op jit(solution)/shard_map/erd,edf->erf/dot_general | solution.py:21
  521.6 27.3 %convolution_convert_fusion.2 = bf16[4,1024,2048]{2,1,0:T(8,128)(2,1)} fusion(bf16[4,1024,1024]{2,1,0:T(8,128)(2,1)} %multiply_convert_fusion, bf16[4,1024,2048]{2,1,0:T(8,128)(2,1)} %param.23), kind=kOutput, calls=%fused_computation.14 | convolution fusion | flops 17188257792 | bytes 41943040 | tf_op jit(solution)/shard_map/erf,efd->erd/dot_general | solution.py:23
  548.9 14.1 copy.75
  563.0 272.2 %all-to-all-done = bf16[4,16,64,2048]{3,2,0,1:T(8,128)(2,1)} async-done(((bf16[4,16,64,2048]{3,2,0,1:T(8,128)(2,1)}), bf16[4,16,64,2048]{3,2,0,1:T(8,128)(2,1)}, u32[]{:S(2)}, u32[]{:S(2)}) %all-to-all-start) | async-done | bytes 16777248 | tf_op jit(solution)/shard_map/all_to_all | solution.py:38
  835.2 7.4 all-to-all-start.3
  842.6 8.1 copy.65
  850.7 5.7 copy-done.4
  856.4 22.2 %fusion.69 = f32[4,1024,1024]{2,1,0:T(8,128)} fusion(bf16[4,1024,2048]{2,1,0:T(8,128)(2,1)S(1)} %bitcast.214, bf16[4,2048,1024]{2,1,0:T(8,128)(2,1)} %param.21), kind=kOutput, calls=%fused_computation.115 | convolution fusion | flops 17179869184 | bytes 50331648 | tf_op jit(solution)/shard_map/erd,edf->erf/dot_general | solution.py:20
  878.6 29.8 %multiply_convert_fusion.1 = bf16[4,1024,1024]{2,1,0:T(8,128)(2,1)} fusion(f32[4,1024,1024]{2,1,0:T(8,128)} %fusion.69, bf16[4,1024,2048]{2,1,0:T(8,128)(2,1)} %bitcast.215, bf16[4,2048,1024]{2,1,0:T(8,128)(2,1)} %param.22), kind=kOutput, calls=%fused_computation.10 | convolution fusion | flops 17205035008 | bytes 58720256 | tf_op jit(solution)/shard_map/erd,edf->erf/dot_general | solution.py:21
  908.4 27.2 %convolution_convert_fusion.3 = bf16[4,1024,2048]{2,1,0:T(8,128)(2,1)} fusion(bf16[4,1024,1024]{2,1,0:T(8,128)(2,1)} %multiply_convert_fusion.1, bf16[4,1024,2048]{2,1,0:T(8,128)(2,1)} %param.23), kind=kOutput, calls=%fused_computation.15 | convolution fusion | flops 17188257792 | bytes 41943040 | tf_op jit(solution)/shard_map/erf,efd->erd/dot_general | solution.py:23
  935.6 14.1 copy.66
  949.7 272.3 %all-to-all-done.3 = bf16[4,16,64,2048]{3,2,0,1:T(8,128)(2,1)} async-done(((bf16[4,16,64,2048]{3,2,0,1:T(8,128)(2,1)}), bf16[4,16,64,2048]{3,2,0,1:T(8,128)(2,1)}, u32[]{:S(2)}, u32[]{:S(2)}) %all-to-all-start.3) | async-done | bytes 16777248 | tf_op jit(solution)/shard_map/all_to_all | solution.py:40
  1222.0 6.6 all-to-all-start.1
  1228.7 12.7 convolution_convert_fusion.4
  1241.4 14.1 copy.76
  1255.5 40.1 %fusion = f32[256,8,2048]{2,0,1:T(8,128)} fusion(bf16[4096,2048,1]{1,0,2:T(8,128)(2,1)} %bitcast.216, s32[256,8]{0,1:T(8,128)S(1)} %copy-done.8), kind=kOutput, calls=%fused_computation.1 | convolution fusion | flops 34368126976 | bytes 33562624 | tf_op jit(solution)/shard_map/tjs,sd->tjd/dot_general | solution.py:41
  1295.6 312.8 %all-to-all-done.1 = bf16[4,16,64,2048]{3,2,0,1:T(8,128)(2,1)} async-done(((bf16[4,16,64,2048]{3,2,0,1:T(8,128)(2,1)}), bf16[4,16,64,2048]{3,2,0,1:T(8,128)(2,1)}, u32[]{:S(2)}, u32[]{:S(2)}) %all-to-all-start.1) | async-done | bytes 16777248 | tf_op jit(solution)/shard_map/all_to_all | solution.py:40
  1608.3 14.1 copy.67
  1622.5 40.2 %fusion.2 = f32[256,8,2048]{2,0,1:T(8,128)} fusion(bf16[4096,2048,1]{1,0,2:T(8,128)(2,1)} %bitcast.217, s32[256,8]{0,1:T(8,128)S(1)} %copy-done.10), kind=kOutput, calls=%fused_computation.4 | convolution fusion | flops 34368126976 | bytes 33562624 | tf_op jit(solution)/shard_map/tjs,sd->tjd/dot_general | solution.py:41
  1662.6 7.7 fusion.14
  1670.3 3.3 copy-done.2
  1673.6 0.2 copy-done.5
  1673.9 2.4 fusion.31
  (26 shorter events, 0.2 us)
Async XLA Ops:
  0.6 26.9 %copy-start = (bf16[256,2048]{1,0:T(8,128)(2,1)S(1)}, bf16[256,2048]{1,0:T(8,128)(2,1)}, u32[]{:S(2)}) copy-start(bf16[256,2048]{1,0:T(8,128)(2,1)} %param.16) | copy-start | bytes 3145732
  22.1 0.6 copy-start.7
  57.9 11.4 copy-start.11
  57.9 390.7 %all-to-all-start.2 = ((bf16[4,16,64,2048]{3,2,0,1:T(8,128)(2,1)}), bf16[4,16,64,2048]{3,2,0,1:T(8,128)(2,1)}, u32[]{:S(2)}, u32[]{:S(2)}) async-start(bf16[4,16,64,2048]{3,2,0,1:T(8,128)(2,1)} %copy.73), calls=%async_computation.2 | async-start | bytes 33554432 | tf_op jit(solution)/shard_map/all_to_all | solution.py:38
  89.3 28.3 %copy-start.9 = (s32[256,8]{0,1:T(8,128)}, s32[256,8]{0,1:T(8,128)S(1)}, u32[]{:S(2)}) copy-start(s32[256,8]{0,1:T(8,128)S(1)} %fusion.53) | copy-start | bytes 24580
  448.6 386.5 %all-to-all-start = ((bf16[4,16,64,2048]{3,2,0,1:T(8,128)(2,1)}), bf16[4,16,64,2048]{3,2,0,1:T(8,128)(2,1)}, u32[]{:S(2)}, u32[]{:S(2)}) async-start(bf16[4,16,64,2048]{3,2,0,1:T(8,128)(2,1)} %copy.64), calls=%async_computation | async-start | bytes 33554432 | tf_op jit(solution)/shard_map/all_to_all | solution.py:38
  463.9 5.7 copy-start.3
  835.2 386.8 %all-to-all-start.3 = ((bf16[4,16,64,2048]{3,2,0,1:T(8,128)(2,1)}), bf16[4,16,64,2048]{3,2,0,1:T(8,128)(2,1)}, u32[]{:S(2)}, u32[]{:S(2)}) async-start(bf16[4,16,64,2048]{3,2,0,1:T(8,128)(2,1)} %copy.75), calls=%async_computation.3 | async-start | bytes 33554432 | tf_op jit(solution)/shard_map/all_to_all | solution.py:40
  850.7 5.7 copy-start.4
  949.7 278.9 %copy-start.12 = (f32[256,8]{0,1:T(8,128)S(1)}, f32[256,8]{0,1:T(8,128)}, u32[]{:S(2)}) copy-start(f32[256,8]{0,1:T(8,128)} %param.18) | copy-start | bytes 24580
  949.7 278.9 %copy-start.13 = (f32[256,8]{0,1:T(8,128)S(1)}, f32[256,8]{0,1:T(8,128)}, u32[]{:S(2)}) copy-start(f32[256,8]{0,1:T(8,128)} %param.14) | copy-start | bytes 24580
  949.7 278.9 %copy-start.14 = (bf16[256,2048]{1,0:T(8,128)(2,1)S(1)}, bf16[256,2048]{1,0:T(8,128)(2,1)}, u32[]{:S(2)}) copy-start(bf16[256,2048]{1,0:T(8,128)(2,1)} %param.15) | copy-start | bytes 3145732
  1222.0 386.4 %all-to-all-start.1 = ((bf16[4,16,64,2048]{3,2,0,1:T(8,128)(2,1)}), bf16[4,16,64,2048]{3,2,0,1:T(8,128)(2,1)}, u32[]{:S(2)}, u32[]{:S(2)}) async-start(bf16[4,16,64,2048]{3,2,0,1:T(8,128)(2,1)} %copy.66), calls=%async_computation.1 | async-start | bytes 33554432 | tf_op jit(solution)/shard_map/all_to_all | solution.py:40
  1241.4 14.1 copy-start.8
  1295.6 326.9 %copy-start.10 = (s32[256,8]{0,1:T(8,128)S(1)}, s32[256,8]{0,1:T(8,128)}, u32[]{:S(2)}) copy-start(s32[256,8]{0,1:T(8,128)} %copy-done.9) | copy-start | bytes 24580
  1622.4 40.2 %copy-start.6 = (bf16[256,2048]{1,0:T(8,128)(2,1)S(1)}, bf16[256,2048]{1,0:T(8,128)(2,1)}, u32[]{:S(2)}) copy-start(bf16[256,2048]{1,0:T(8,128)(2,1)} %fusion.10) | copy-start | bytes 3145732
  1662.6 11.0 copy-start.2
  1662.6 11.2 copy-start.5
  1662.6 13.6 copy-start.1
where the time goes:
time: 1690 us; the launch traced here: 1680 us
  waiting for transfers between devices  1190 us (70%)
  matrix products  277 us (16%)
  local copies, waits for them, and re-layouts  120 us (7%)
  other arithmetic  58 us (3%)
  starting transfers between devices  32.6 us (2%)
    all_to_all x2, waiting for transfers between devices, moe_local(): recv_buf = lax.all_to_all(send_buf, 'ep', 1, 1, tiled=True)  603 us
    all_to_all x2, waiting for transfers between devices, moe_local(): lax.all_to_all(expert_out.reshape(local_n, n_devs, capacity, model_dim),...  585 us
    dot_general x2, matrix products, moe_local(): jnp.einsum('tjs,sd->tjd', picker, back_buf.reshape(n_slots, model_dim), p...  80.2 us
    dot_general x2, matrix products, expert_ffn(): jnp.einsum('erd,edf->erf', rows_in, w_up, preferred_element_type=jnp.floa...  59.6 us
    dot_general x2, matrix products, expert_ffn(): jnp.einsum('erf,efd->erd', hidden, w_down, preferred_element_type=jnp.flo...  54.4 us
    dot_general x2, matrix products, expert_ffn(): jnp.einsum('erd,edf->erf', rows_in, w_gate, preferred_element_type=jnp.fl...  44.4 us
    another operation x4, other arithmetic  36.7 us
  transfers between devices with their start and end apart: 4, of which 4 were waited for; matrix products, arithmetic and copies ran while one was open for 19% of the time, Pallas kernels for 0%

commit v1 on v0

v1 whole, which is shorter than its diff:
```python
import functools

import jax
import jax.numpy as jnp
from jax import lax
from jax.experimental import pallas as pl
from jax.experimental.pallas import tpu as pltpu
from jax.sharding import PartitionSpec as P

CORES = 2


def slot_tables(route_all, gate_all, expert_ids):
    n_src, tok_n, top_k = route_all.shape
    route_t = jnp.swapaxes(route_all, 1, 2)
    gate_t = jnp.swapaxes(gate_all, 1, 2)
    hit = route_t[:, :, None, :] == expert_ids[None, None, :, None]
    chosen = jnp.any(hit, axis=1)
    gate = jnp.sum(jnp.where(hit, gate_t[:, :, None, :], 0.0), axis=1)
    before = (jnp.arange(tok_n)[:, None] < jnp.arange(tok_n)[None, :]).astype(jnp.bfloat16)
    rank = jnp.einsum('set,tu->seu', chosen.astype(jnp.bfloat16), before, preferred_element_type=jnp.float32)
    rank = jnp.where(chosen, rank.astype(jnp.int32), -1)
    return rank, jnp.swapaxes(rank, 1, 2), jnp.swapaxes(gate, 1, 2)


def moe_kernel(n_src, local_n, capacity, rank_ref, rank_t_ref, gate_ref, x_ref, *refs):
    own, peer = refs[0:3], refs[3:6]
    out_ref, rows_ref = refs[6], refs[7]
    bufs, sems = refs[8:11], refs[11]
    n_exp = CORES * local_n
    step = pl.program_id(0)
    tok_n, model_dim = x_ref.shape[1:]

    def load(side, idx, slot):
        for k in range(3):
            pltpu.make_async_copy(side[k].at[idx], bufs[k].at[slot], sems.at[slot, k]).start()

    @pl.when(step == 0)
    def _():
        load(own, 0, 0)
        load(own, 1, 1)

    @pl.when(step < n_src)
    def _():
        slot_no = lax.broadcasted_iota(jnp.int32, (capacity, tok_n), 0)
        picks = [jnp.where(slot_no == rank_ref[0, e : e + 1, :], 1.0, 0.0) for e in range(n_exp)]
        place = jnp.concatenate(picks, axis=0).astype(jnp.bfloat16)
        rows_ref[step] = jnp.dot(place, x_ref[0], preferred_element_type=jnp.float32).astype(jnp.bfloat16)

    @pl.when(jnp.logical_and(step >= n_src, step < n_src + n_exp))
    def _():
        e = step - n_src
        slot = lax.rem(e, 2)
        for k in range(3):
            pltpu.make_async_copy(own[k].at[0], bufs[k].at[slot], sems.at[slot, k]).wait()
        at = pl.ds(pl.multiple_of(e * capacity, capacity), capacity)
        rows = rows_ref[:, at, :].reshape(n_src * capacity, model_dim)
        gate_act = jnp.dot(rows, bufs[0][slot], preferred_element_type=jnp.float32)
        up_act = jnp.dot(rows, bufs[1][slot], preferred_element_type=jnp.float32)
        hidden = (gate_act * jax.nn.sigmoid(gate_act) * up_act).astype(jnp.bfloat16)
        y = jnp.dot(hidden, bufs[2][slot], preferred_element_type=jnp.float32).astype(jnp.bfloat16)
        rows_ref[:, at, :] = y.reshape(n_src, capacity, model_dim)

        @pl.when(e + 2 < local_n)
        def _():
            load(own, e + 2, slot)

        @pl.when(jnp.logical_and(e + 2 >= local_n, e + 2 < n_exp))
        def _():
            load(peer, e + 2 - local_n, slot)

    @pl.when(step >= n_src + n_exp)
    def _():
        src = step - n_src - n_exp
        col = lax.broadcasted_iota(jnp.int32, (tok_n, capacity), 1)
        parts = []
        for e in range(n_exp):
            parts.append(jnp.where(col == rank_t_ref[0, :, e : e + 1], gate_ref[0, :, e : e + 1], 0.0))
        weight = jnp.concatenate(parts, axis=1)
        hi = weight.astype(jnp.bfloat16)
        rest = weight - hi.astype(jnp.float32)
        mid = rest.astype(jnp.bfloat16)
        lo = (rest - mid.astype(jnp.float32)).astype(jnp.bfloat16)
        y = rows_ref[src]
        total = jnp.dot(hi, y, preferred_element_type=jnp.float32)
        total += jnp.dot(mid, y, preferred_element_type=jnp.float32)
        total += jnp.dot(lo, y, preferred_element_type=jnp.float32)
        out_ref[0] = total


def expert_sums(rows_all, tables, own, peer):
    n_src, tok_n, model_dim = rows_all.shape
    local_n, _, ff_dim = own[0].shape
    n_exp = CORES * local_n
    rank, rank_t, gate = tables
    n_devs = n_src * CORES
    capacity = min(tok_n, 2 * ((tok_n * 8 + n_devs * local_n - 1) // (n_devs * local_n)))
    first = lambda i: (jnp.minimum(i, n_src - 1), 0, 0)
    last = lambda i: (jnp.clip(i - n_src - n_exp, 0, n_src - 1), 0, 0)
    any_spec = pl.BlockSpec(memory_space=pl.ANY)
    slots = n_exp * capacity
    flops = n_src * slots * model_dim * (6 * ff_dim + 2 * tok_n * 4)
    return pl.pallas_call(
        functools.partial(moe_kernel, n_src, local_n, capacity),
        grid=(n_src + n_exp + n_src,),
        out_shape=jax.ShapeDtypeStruct((n_src, tok_n, model_dim), jnp.float32),
        in_specs=[
            pl.BlockSpec((1, n_exp, tok_n), first),
            pl.BlockSpec((1, tok_n, n_exp), last),
            pl.BlockSpec((1, tok_n, n_exp), last),
            pl.BlockSpec((1, tok_n, model_dim), first),
        ]
        + [any_spec] * 6,
        out_specs=pl.BlockSpec((1, tok_n, model_dim), last),
        scratch_shapes=[
            pltpu.VMEM((n_src, slots, model_dim), jnp.bfloat16),
            pltpu.VMEM((2, model_dim, ff_dim), jnp.bfloat16),
            pltpu.VMEM((2, model_dim, ff_dim), jnp.bfloat16),
            pltpu.VMEM((2, ff_dim, model_dim), jnp.bfloat16),
            pltpu.SemaphoreType.DMA((2, 3)),
        ],
        compiler_params=pltpu.CompilerParams(
            dimension_semantics=('arbitrary',), vmem_limit_bytes=62 * 1024 * 1024
        ),
        cost_estimate=pl.CostEstimate(flops=flops, bytes_accessed=160 * 2**20, transcendentals=0),
    )(rank, rank_t, gate, rows_all, *own, *peer)


def solution(mesh):
    n_devs = mesh.shape['ep']
    groups = [list(range(c, n_devs, CORES)) for c in range(CORES)]
    swap = [(d, d ^ 1) for d in range(n_devs)]

    def gather(vals):
        return lax.all_gather(vals, 'ep', axis_index_groups=groups)

    def local_step(x_a, route_a, gate_a, h_b, attn_b, route_b, gate_b, w_qkv, w_o, w_gate, w_up, w_down):
        k = route_a.shape[1]
        local_n = w_gate.shape[0]
        me = lax.axis_index('ep')
        own = (w_gate, w_up, w_down)
        rows_a = gather(x_a)
        peer = tuple(lax.ppermute(w, 'ep', swap) for w in own)
        proj_b = jnp.dot(attn_b, w_o, preferred_element_type=jnp.float32).astype(jnp.bfloat16)
        mid_b = (h_b.astype(jnp.float32) + proj_b.astype(jnp.float32)).astype(jnp.bfloat16)
        rows_a, sent_b = lax.optimization_barrier((rows_a, mid_b))
        rows_b = gather(sent_b)
        meta = jnp.concatenate([route_a.astype(jnp.float32), gate_a, route_b.astype(jnp.float32), gate_b], axis=1)
        meta = gather(meta)
        ids = meta.astype(jnp.int32)
        local = jnp.arange(local_n)
        expert_ids = jnp.concatenate([me * local_n + local, (me ^ 1) * local_n + local])
        tables_a = slot_tables(ids[:, :, :k], meta[:, :, k : 2 * k], expert_ids)
        tables_b = slot_tables(ids[:, :, 2 * k : 3 * k], meta[:, :, 3 * k :], expert_ids)
        part_a = expert_sums(rows_a, tables_a, own, peer)
        sum_a = lax.psum_scatter(part_a, 'ep', axis_index_groups=groups)
        part_b = expert_sums(rows_b, tables_b, own, peer)
        sum_b = lax.psum_scatter(part_b, 'ep', axis_index_groups=groups)
        qkv_b = jnp.dot(h_b, w_qkv, preferred_element_type=jnp.float32).astype(jnp.bfloat16)
        out_a = (x_a.astype(jnp.float32) + sum_a).astype(jnp.bfloat16)
        out_b = (mid_b.astype(jnp.float32) + sum_b).astype(jnp.bfloat16)
        return out_a, out_b, qkv_b

    row_spec = P(('dp', 'ep'), None)
    full_spec = P(None, None)
    expert_spec = P('ep', None, None)
    return jax.shard_map(
        local_step,
        mesh=mesh,
        in_specs=(row_spec, row_spec, row_spec, row_spec, row_spec, row_spec, row_spec, full_spec, full_spec, expert_spec, expert_spec, expert_spec),
        out_specs=(row_spec, row_spec, row_spec),
        check_vma=False,
    )
```

time: 1690 us -> 578 us (0.34)
  waiting for transfers between devices: 1190 us -> 317 us
  matrix products: 277 us -> 20.9 us
  Pallas kernels: 0 us -> 187 us
  local copies, waits for them, and re-layouts: 120 us -> 5.7 us
  other arithmetic: 58 us -> 6.2 us
  starting transfers between devices: 32.6 us -> 5.74 us
  blocking collectives: 0 us -> 21 us
    all_to_all x4 -> x0, waiting for transfers between devices: 1190 us -> none  [the longest x2 603 us: moe_local(): recv_buf = lax.all_to_all(send_buf, 'ep', 1, 1, tiled=True)]
    dot_general x10 -> x2, matrix products: 257 us -> 0.76 us  [slot_tables(): jnp.einsum('set,tu->seu', chosen.astype(jnp.bfloat16), before, preferred_...]
    reduce_scatter x0 -> x2, waiting for transfers between devices: none -> 232 us  [the longest x1 168 us: local_step(): sum_b = lax.psum_scatter(part_b, 'ep', axis_index_groups=groups)]
    pallas_call x0 -> x2, Pallas kernels: none -> 187 us  [expert_sums(): pl.pallas_call(functools.partial(moe_kernel, n_src, local_n, capacity), g...]
    all_gather x0 -> x2, waiting for transfers between devices: none -> 84.4 us  [gather(): return lax.all_gather(vals, 'ep', axis_index_groups=groups)]
    reshape x4 -> x0, local copies, waits for them, and re-layouts: 56.4 us -> none  [the longest x2 28.2 us: moe_local(): expert_out.reshape(local_n, n_devs, capacity, model_dim)]
    all_to_all x4 -> x0, local copies, waits for them, and re-layouts: 44.4 us -> none  [the longest x2 28.2 us: moe_local(): lax.all_to_all(expert_out.reshape(local_n, n_devs, capacity, model_dim),...]
    another operation x4 -> x0, other arithmetic: 36.7 us -> none
  transfers between devices with their start and end apart: 4 -> 7, of which waited for: 4 -> 3; matrix products, arithmetic and copies ran while one was open for 19% -> 5% of each run, Pallas kernels for 0% -> 32%
where the time goes in v1:
time: 578 us
  waiting for transfers between devices  317 us (55%)
  Pallas kernels  187 us (32%)
  blocking collectives  21 us (4%)
  matrix products  20.9 us (4%)
  between operations  14.1 us (2%)
  other arithmetic  6.2 us (1%)
    pallas_call x2, Pallas kernels, expert_sums(): pl.pallas_call(functools.partial(moe_kernel, n_src, local_n, capacity), g...  187 us
    reduce_scatter x1, waiting for transfers between devices, local_step(): sum_b = lax.psum_scatter(part_b, 'ep', axis_index_groups=groups)  168 us
    all_gather x2, waiting for transfers between devices, gather(): return lax.all_gather(vals, 'ep', axis_index_groups=groups)  84.4 us
    reduce_scatter x1, waiting for transfers between devices, local_step(): sum_a = lax.psum_scatter(part_a, 'ep', axis_index_groups=groups)  63.7 us
    all_gather x1, blocking collectives, gather(): return lax.all_gather(vals, 'ep', axis_index_groups=groups)  21 us
    dot_general x1, matrix products, local_step(): jnp.dot(h_b, w_qkv, preferred_element_type=jnp.float32).astype(jnp.bfloat16)  13.2 us
  transfers between devices with their start and end apart: 7, of which 3 were waited for; matrix products, arithmetic and copies ran while one was open for 5% of the time, Pallas kernels for 32%

profile of v1, /device:TPU:21, one launch (start us, length us, event | category | flops | bytes accessed | tf_op | source)
XLA Modules:
  0.0 577.9 jit_solution(13014694131181807052)
XLA Ops:
  7.2 0.0 copy-start
  7.2 0.1 all-gather.6.cloned.1.call-start
  7.3 0.7 all-gather.6.cloned.1.call-update
  8.0 0.0 copy-start.6
  8.0 0.0 copy-start.7
  8.0 0.0 copy-start.8
  8.0 0.0 copy-start.9
  8.0 0.1 all-gather.8.cloned.1.call-start
  8.1 4.8 collective-permute-start
  12.9 0.1 collective-permute-start.1
  13.0 0.4 collective-permute-start.2
  13.4 0.0 copy-done
  13.4 6.9 %fusion.2 = bf16[256,2048]{1,0:T(8,128)(2,1)} fusion(bf16[256,2048]{1,0:T(8,128)(2,1)S(1)} %copy-done, bf16[2048,2048]{1,0:T(8,128)(2,1)} %param.20, bf16[256,2048]{1,0:T(8,128)(2,1)} %param.15), kind=kOutput, calls=%fused_computation.4 | convolution fusion | flops 2150105088 | bytes 11534336 | tf_op jit(solution)/shard_map/dot_general | solution.py:144
  20.3 84.4 %all-gather.6.cloned.1.call-done = bf16[2048,2048]{1,0:T(8,128)(2,1)} async-done(((bf16[256,2048]{1,0:T(8,128)(2,1)}), bf16[2048,2048]{1,0:T(8,128)(2,1)}) %all-gather.6.cloned.1.call-update) | async-done | bytes 8388624 | tf_op jit(solution)/shard_map/all_gather | solution.py:135
  104.7 0.1 all-gather.8.cloned.1.call-update
  104.8 0.1 reduce-scatter.3.cloned.1.call-start
  104.9 0.0 copy-done.6
  104.9 0.0 copy-done.7
  104.9 0.0 copy-done.8
  104.9 0.0 copy-done.9
  104.9 21.0 %all-gather = f32[2048,32]{0,1:T(8,128)S(1)} all-gather(f32[256,32]{0,1:T(8,128)S(1)} %pad_maximum_fusion), channel_id=2, replica_groups={{0,2,4,6,8,10,12,14},{1,3,5,7,9,11,13,15},{16,18,20,22,24,26,28,30},{17..., dimensions={0}, use_global_device_ids=true | all-gather | bytes 294912 | tf_op jit(solution)/shard_map/all_gather | solution.py:135
  126.0 0.1 copy.39
  126.2 0.1 pad_add_fusion
  126.3 0.2 compare_reduce_fusion
  126.5 0.4 copy.27
  126.9 0.4 fusion.5
  127.3 0.0 copy-start.4
  127.3 1.0 copy.30.rank_ref
  128.3 0.0 copy-done.4
  128.4 0.2 fusion.8
  128.6 1.3 copy.29
  129.9 0.0 collective-permute-done.refs_3_
  129.9 0.0 collective-permute-done.1.refs_4_
  129.9 0.0 collective-permute-done.2.refs_5_
  129.9 93.5 %shard_map.139 = f32[8,256,2048]{2,1,0:T(8,128)} custom-call(s32[8,8,256]{2,1,0:T(8,128)} %copy.30.rank_ref, s32[8,256,8]{2,1,0:T(8,128)} %bitcast.38, f32[8,256,8]{2,1,0:T(8,128)} %bitcast.39, bf16[8,256,2048]{2,1,0:T(8,128)(2,1)} %bitcast.44, bf16[4,2048,1024]{2,1,0:T(8,128)(2,1)} %refs_0_.3, bf16[4,2048,1024]{2,1,0:T(8,128)(2,1)} %refs_1_.3, ...), custom_call_target="tpu_custom_call" | custom-call | flops 68719476736 | bytes 167772160 | tf_op jit(solution)/shard_map/pallas_call | solution.py:103
  223.4 0.1 reduce-scatter.3.cloned.1.call-update
  223.5 0.3 reduce-scatter.5.cloned.1.call-start
  223.7 0.4 copy.33
  224.2 0.4 fusion.6
  224.6 0.0 copy-start.5
  224.6 1.0 copy.36.rank_ref
  225.6 1.3 copy.35
  226.9 0.0 all-gather.8.cloned.1.call-done
  226.9 0.0 copy-done.5
  226.9 93.4 %shard_map.140 = f32[8,256,2048]{2,1,0:T(8,128)} custom-call(s32[8,8,256]{2,1,0:T(8,128)} %copy.36.rank_ref, s32[8,256,8]{2,1,0:T(8,128)} %bitcast.40, f32[8,256,8]{2,1,0:T(8,128)} %bitcast.41, bf16[8,256,2048]{2,1,0:T(8,128)(2,1)} %bitcast.43, bf16[4,2048,1024]{2,1,0:T(8,128)(2,1)} %refs_0_.3, bf16[4,2048,1024]{2,1,0:T(8,128)(2,1)} %refs_1_.3, ...), custom_call_target="tpu_custom_call" | custom-call | flops 68719476736 | bytes 167772160 | tf_op jit(solution)/shard_map/pallas_call | solution.py:103
  320.3 0.1 reduce-scatter.5.cloned.1.call-update
  320.4 0.0 copy-start.2
  320.4 0.0 copy-start.3
  320.4 0.0 copy-start.1
  320.4 13.2 %convolution_convert_fusion = bf16[256,6144]{1,0:T(8,128)(2,1)} fusion(bf16[256,2048]{1,0:T(8,128)(2,1)} %param.15, bf16[2048,6144]{1,0:T(8,128)(2,1)} %param.19), kind=kOutput, calls=%fused_computation | convolution fusion | flops 6444023808 | bytes 29360128 | tf_op jit(solution)/shard_map/dot_general | solution.py:159
  333.6 63.7 %reduce-scatter.3.cloned.1.call-done = f32[1,256,2048]{2,1,0:T(8,128)} async-done(((f32[8,256,2048]{2,1,0:T(8,128)}), f32[1,256,2048]{2,1,0:T(8,128)}) %reduce-scatter.3.cloned.1.call-update) | async-done | bytes 2097168 | tf_op jit(solution)/shard_map/reduce_scatter | solution.py:156
  397.3 0.0 copy-done.2
  397.3 2.8 fusion.4
  400.1 168.3 %reduce-scatter.5.cloned.1.call-done = f32[1,256,2048]{2,1,0:T(8,128)} async-done(((f32[8,256,2048]{2,1,0:T(8,128)}), f32[1,256,2048]{2,1,0:T(8,128)}) %reduce-scatter.5.cloned.1.call-update) | async-done | bytes 2097168 | tf_op jit(solution)/shard_map/reduce_scatter | solution.py:158
  568.5 0.0 copy-done.3
  568.5 2.8 fusion.3
  571.3 0.0 copy-done.1
  (11 shorter events, 0.2 us)
Async XLA Ops:
  7.2 6.2 %copy-start = (bf16[256,2048]{1,0:T(8,128)(2,1)S(1)}, bf16[256,2048]{1,0:T(8,128)(2,1)}, u32[]{:S(2)}) copy-start(bf16[256,2048]{1,0:T(8,128)(2,1)} %param.16) | copy-start | bytes 3145732
  7.2 97.5 %all-gather.6.cloned.1.call-start = ((), (), s32[]{:S(2)}) async-start(), calls=%async_computation.4 | async-start | bytes 9437184 | tf_op jit(solution)/shard_map/all_gather | solution.py:135
  8.0 96.9 %copy-start.6 = (s32[256,8]{0,1:T(8,128)S(1)}, s32[256,8]{0,1:T(8,128)}, u32[]{:S(2)}) copy-start(s32[256,8]{0,1:T(8,128)} %param.17) | copy-start | bytes 24580
  8.0 96.9 %copy-start.7 = (s32[256,8]{0,1:T(8,128)S(1)}, s32[256,8]{0,1:T(8,128)}, u32[]{:S(2)}) copy-start(s32[256,8]{0,1:T(8,128)} %param.13) | copy-start | bytes 24580
  8.0 96.9 %copy-start.8 = (f32[256,8]{0,1:T(8,128)S(1)}, f32[256,8]{0,1:T(8,128)}, u32[]{:S(2)}) copy-start(f32[256,8]{0,1:T(8,128)} %param.18) | copy-start | bytes 24580
  8.0 96.9 %copy-start.9 = (f32[256,8]{0,1:T(8,128)S(1)}, f32[256,8]{0,1:T(8,128)}, u32[]{:S(2)}) copy-start(f32[256,8]{0,1:T(8,128)} %param.14) | copy-start | bytes 24580
  8.0 218.8 %all-gather.8.cloned.1.call-start = ((), (), s32[]{:S(2)}) async-start(), calls=%async_computation.5 | async-start | bytes 9437184 | tf_op jit(solution)/shard_map/all_gather | solution.py:135
  8.1 121.8 %collective-permute-start = (bf16[4,2048,1024]{2,1,0:T(8,128)(2,1)}, bf16[4,2048,1024]{2,1,0:T(8,128)(2,1)}, u32[]{:S(2)}, u32[]{:S(2)}) collective-permute-start(bf16[4,2048,1024]{2,1,0:T(8,128)(2,1)} %refs_0_.3), channel_id=1, source_target_pairs={{0,1},{1,0},{2,3},{3,2},{4,5},{5,4},{6,7},{7,6},{8,9},{9,8},{10,11... | collective-permute-start | bytes 50331656 | tf_op jit(solution)/shard_map/ppermute | solution.py:143
  12.9 117.0 %collective-permute-start.1 = (bf16[4,2048,1024]{2,1,0:T(8,128)(2,1)}, bf16[4,2048,1024]{2,1,0:T(8,128)(2,1)}, u32[]{:S(2)}, u32[]{:S(2)}) collective-permute-start(bf16[4,2048,1024]{2,1,0:T(8,128)(2,1)} %refs_1_.3), channel_id=1, source_target_pairs={{0,1},{1,0},{2,3},{3,2},{4,5},{5,4},{6,7},{7,6},{8,9},{9,8},{10,11... | collective-permute-start | bytes 50331656 | tf_op jit(solution)/shard_map/ppermute | solution.py:143
  13.0 116.9 %collective-permute-start.2 = (bf16[4,1024,2048]{2,1,0:T(8,128)(2,1)}, bf16[4,1024,2048]{2,1,0:T(8,128)(2,1)}, u32[]{:S(2)}, u32[]{:S(2)}) collective-permute-start(bf16[4,1024,2048]{2,1,0:T(8,128)(2,1)} %refs_2_.3), channel_id=1, source_target_pairs={{0,1},{1,0},{2,3},{3,2},{4,5},{5,4},{6,7},{7,6},{8,9},{9,8},{10,11... | collective-permute-start | bytes 50331656 | tf_op jit(solution)/shard_map/ppermute | solution.py:143
  104.8 292.5 %reduce-scatter.3.cloned.1.call-start = ((), (), s32[]{:S(2)}) async-start(), calls=%async_computation.2 | async-start | bytes 18874368 | tf_op jit(solution)/shard_map/reduce_scatter | solution.py:156
  127.3 1.0 copy-start.4
  223.5 345.0 %reduce-scatter.5.cloned.1.call-start = ((), (), s32[]{:S(2)}) async-start(), calls=%async_computation.3 | async-start | bytes 18874368 | tf_op jit(solution)/shard_map/reduce_scatter | solution.py:158
  224.6 2.3 copy-start.5
  320.4 76.9 %copy-start.2 = (bf16[256,2048]{1,0:T(8,128)(2,1)S(1)}, bf16[256,2048]{1,0:T(8,128)(2,1)}, u32[]{:S(2)}) copy-start(bf16[256,2048]{1,0:T(8,128)(2,1)} %param.12) | copy-start | bytes 3145732
  320.4 248.1 %copy-start.3 = (bf16[256,2048]{1,0:T(8,128)(2,1)S(1)}, bf16[256,2048]{1,0:T(8,128)(2,1)}, u32[]{:S(2)}) copy-start(bf16[256,2048]{1,0:T(8,128)(2,1)} %fusion.2) | copy-start | bytes 3145732
  320.4 250.9 %copy-start.1 = (bf16[256,2048]{1,0:T(8,128)(2,1)S(1)}, bf16[256,2048]{1,0:T(8,128)(2,1)}, u32[]{:S(2)}) copy-start(bf16[256,2048]{1,0:T(8,128)(2,1)} %param.16) | copy-start | bytes 3145732
Sparse Core Ops, SparseCore 0:
  9.6 95.0 all-gather.5
  106.3 90.7 all-gather.7
  223.6 173.6 reduce-scatter.2
  399.5 168.8 reduce-scatter.4

commit v2 on v1

--- a/solution.py
+++ b/solution.py
@@ -126,6 +126,104 @@
     )(rank, rank_t, gate, rows_all, *own, *peer)
 
 
+def ring_kernel(n_src, n_devs, part_ref, mid_ref, out_ref, local, slots, load_sems, send_sems, recv_sems):
+    tok_n, model_dim = mid_ref.shape
+    rows_n, cols_n = tok_n // 2, model_dim // 2
+    me = lax.axis_index('ep')
+    pos = lax.div(me, CORES)
+    to = {1: lax.rem(me + CORES, n_devs), -1: lax.rem(me + n_devs - CORES, n_devs)}
+
+    barrier = pltpu.get_barrier_semaphore()
+    for way in (1, -1):
+        pl.semaphore_signal(barrier, inc=1, device_id={'ep': to[way]}, device_id_type=pl.DeviceIdType.MESH)
+    pl.semaphore_wait(barrier, 2)
+
+    far = n_src // 2
+    near = n_src - 1 - far
+    chains = []
+    for dist, pairs in ((far, ((1, 0), (-1, 1))), (near, ((1, 1), (-1, 0)))):
+        for r in range(2):
+            for way, h in pairs:
+                chains.append((way, r, h, dist))
+    base, count = [], 0
+    for chain in chains:
+        base.append(count)
+        count += chain[3]
+
+    loads = {}
+    order = sorted(range(n_src), key=lambda j: -min(j, n_src - j))
+    for j in order:
+        loads[j] = pltpu.make_async_copy(part_ref.at[lax.rem(pos + j, n_src)], local.at[j], load_sems.at[j])
+        loads[j].start()
+    ready = set()
+
+    def mine(way, dist, r, h):
+        j = (way * dist) % n_src
+        if j not in ready:
+            loads[j].wait()
+            ready.add(j)
+        return local.at[j, pl.ds(r * rows_n, rows_n), pl.ds(h * cols_n, cols_n)]
+
+    copies = {}
+
+    def send(c, hop, src):
+        at = base[c] + hop - 1
+        copies[c, hop] = pltpu.make_async_remote_copy(
+            src_ref=src,
+            dst_ref=slots.at[at],
+            send_sem=send_sems.at[at],
+            recv_sem=recv_sems.at[at],
+            device_id={'ep': to[chains[c][0]]},
+            device_id_type=pl.DeviceIdType.MESH,
+        )
+        copies[c, hop].start()
+
+    for c, (way, r, h, dist) in enumerate(chains):
+        send(c, 1, mine(way, dist, r, h))
+    landed = {}
+    for hop in range(1, far + 1):
+        for c, (way, r, h, dist) in enumerate(chains):
+            if hop > dist:
+                continue
+            copies[c, hop].wait_recv()
+            here = slots.at[base[c] + hop - 1]
+            if hop < dist:
+                here[...] += mine(way, dist - hop, r, h)[...]
+                send(c, hop + 1, here)
+                continue
+            if (r, h) not in landed:
+                landed[r, h] = here
+                continue
+            total = mine(1, 0, r, h)[...] + (landed[r, h][...] + here[...])
+            spot = (pl.ds(r * rows_n, rows_n), pl.ds(h * cols_n, cols_n))
+            out_ref[spot] = (mid_ref[spot].astype(jnp.float32) + total).astype(jnp.bfloat16)
+    for copy in copies.values():
+        copy.wait_send()
+
+
+def ring_sum(part, mid, n_devs):
+    n_src, tok_n, model_dim = part.shape
+    n_slots = 2 * 2 * (n_src - 1)
+    vmem = pl.BlockSpec(memory_space=pltpu.VMEM)
+    return pl.pallas_call(
+        functools.partial(ring_kernel, n_src, n_devs),
+        out_shape=jax.ShapeDtypeStruct((tok_n, model_dim), jnp.bfloat16),
+        in_specs=[pl.BlockSpec(memory_space=pl.ANY), vmem],
+        out_specs=vmem,
+        scratch_shapes=[
+            pltpu.VMEM((n_src, tok_n, model_dim), jnp.float32),
+            pltpu.VMEM((n_slots, tok_n // 2, model_dim // 2), jnp.float32),
+            pltpu.SemaphoreType.DMA((n_src,)),
+            pltpu.SemaphoreType.DMA((n_slots,)),
+            pltpu.SemaphoreType.DMA((n_slots,)),
+        ],
+        compiler_params=pltpu.CompilerParams(
+            collective_id=0, has_side_effects=True, vmem_limit_bytes=56 * 1024 * 1024
+        ),
+        cost_estimate=pl.CostEstimate(flops=80 * 10**9, bytes_accessed=20 * 2**20, transcendentals=0),
+    )(part, mid)
+
+
 def solution(mesh):
     n_devs = mesh.shape['ep']
     groups = [list(range(c, n_devs, CORES)) for c in range(CORES)]
@@ -143,8 +241,6 @@
         peer = tuple(lax.ppermute(w, 'ep', swap) for w in own)
         proj_b = jnp.dot(attn_b, w_o, preferred_element_type=jnp.float32).astype(jnp.bfloat16)
         mid_b = (h_b.astype(jnp.float32) + proj_b.astype(jnp.float32)).astype(jnp.bfloat16)
-        rows_a, sent_b = lax.optimization_barrier((rows_a, mid_b))
-        rows_b = gather(sent_b)
         meta = jnp.concatenate([route_a.astype(jnp.float32), gate_a, route_b.astype(jnp.float32), gate_b], axis=1)
         meta = gather(meta)
         ids = meta.astype(jnp.int32)
@@ -152,13 +248,15 @@
         expert_ids = jnp.concatenate([me * local_n + local, (me ^ 1) * local_n + local])
         tables_a = slot_tables(ids[:, :, :k], meta[:, :, k : 2 * k], expert_ids)
         tables_b = slot_tables(ids[:, :, 2 * k : 3 * k], meta[:, :, 3 * k :], expert_ids)
+        qkv_b = jnp.dot(h_b, w_qkv, preferred_element_type=jnp.float32).astype(jnp.bfloat16)
+        early = (rows_a, mid_b, tables_a, tables_b, qkv_b)
+        rows_a, sent_b, tables_a, tables_b, qkv_b = lax.optimization_barrier(early)
+        rows_b = gather(sent_b)
         part_a = expert_sums(rows_a, tables_a, own, peer)
         sum_a = lax.psum_scatter(part_a, 'ep', axis_index_groups=groups)
         part_b = expert_sums(rows_b, tables_b, own, peer)
-        sum_b = lax.psum_scatter(part_b, 'ep', axis_index_groups=groups)
-        qkv_b = jnp.dot(h_b, w_qkv, preferred_element_type=jnp.float32).astype(jnp.bfloat16)
+        out_b = ring_sum(part_b, mid_b, n_devs)
         out_a = (x_a.astype(jnp.float32) + sum_a).astype(jnp.bfloat16)
-        out_b = (mid_b.astype(jnp.float32) + sum_b).astype(jnp.bfloat16)
         return out_a, out_b, qkv_b
 
     row_spec = P(('dp', 'ep'), None)

time: 578 us -> 540 us (0.934)
  waiting for transfers between devices: 317 us -> 43.5 us
  Pallas kernels: 187 us -> 418 us
    pallas_call x0 -> x1, Pallas kernels: none -> 231 us  [ring_sum(): pl.pallas_call(functools.partial(ring_kernel, n_src, n_devs), out_shape=j...]
    reduce_scatter x1 -> x0, waiting for transfers between devices: 168 us -> none  [local_step(): sum_b = lax.psum_scatter(part_b, 'ep', axis_index_groups=groups)]
    reduce_scatter x1, waiting for transfers between devices: 63.7 us -> 0.02 us  [local_step(): sum_a = lax.psum_scatter(part_a, 'ep', axis_index_groups=groups)]
    all_gather x2, waiting for transfers between devices: 84.4 us -> 42.7 us  [gather(): return lax.all_gather(vals, 'ep', axis_index_groups=groups)]
  transfers between devices with their start and end apart: 7 -> 6, of which waited for: 3 -> 1; matrix products, arithmetic and copies ran while one was open for 5% -> 6% of each run, Pallas kernels for 32% -> 77%
where the time goes in v2:
time: 540 us
  Pallas kernels  418 us (77%)
  waiting for transfers between devices  43.5 us (8%)
  blocking collectives  22.8 us (4%)
  matrix products  21.5 us (4%)
  between operations  14 us (3%)
  local copies, waits for them, and re-layouts  9.16 us (2%)
  starting transfers between devices  5.64 us (1%)
  other arithmetic  5.46 us (1%)
    pallas_call x1, Pallas kernels, ring_sum(): pl.pallas_call(functools.partial(ring_kernel, n_src, n_devs), out_shape=j...  231 us
    pallas_call x2, Pallas kernels, expert_sums(): pl.pallas_call(functools.partial(moe_kernel, n_src, local_n, capacity), g...  187 us
    all_gather x2, waiting for transfers between devices, gather(): return lax.all_gather(vals, 'ep', axis_index_groups=groups)  42.7 us
    all_gather x1, blocking collectives, gather(): return lax.all_gather(vals, 'ep', axis_index_groups=groups)  22.8 us
    dot_general x1, matrix products, local_step(): jnp.dot(h_b, w_qkv, preferred_element_type=jnp.float32).astype(jnp.bfloat16)  12.7 us
  transfers between devices with their start and end apart: 6, of which 1 were waited for; matrix products, arithmetic and copies ran while one was open for 6% of the time, Pallas kernels for 77%

profile of v2, /device:TPU:21, one launch (start us, length us, event | category | flops | bytes accessed | tf_op | source)
XLA Modules:
  0.0 539.8 jit_solution(12848917499288469496)
XLA Ops:
  7.2 0.0 copy-start
  7.2 0.1 all-gather.6.cloned.1.call-start
  7.3 0.7 all-gather.6.cloned.1.call-update
  8.0 0.1 all-gather.8.cloned.1.call-start
  8.1 4.8 collective-permute-start
  12.8 0.1 collective-permute-start.1
  13.0 0.4 collective-permute-start.2
  13.3 0.7 convert_element_type.50
  14.0 0.7 convert_element_type.49
  14.7 0.7 pad_maximum_fusion
  15.4 22.8 %all-gather.1 = f32[2048,32]{0,1:T(8,128)S(1)} all-gather(f32[256,32]{0,1:T(8,128)S(1)} %pad_maximum_fusion), channel_id=3, replica_groups={{0,2,4,6,8,10,12,14},{1,3,5,7,9,11,13,15},{16,18,20,22,24,26,28,30},{17..., dimensions={0}, use_global_device_ids=true | all-gather | bytes 294912 | tf_op jit(solution)/shard_map/all_gather | solution.py:233
  38.3 0.1 copy.39
  38.5 0.1 pad_add_fusion
  38.6 0.2 compare_reduce_fusion
  38.8 0.4 copy.27
  39.3 0.2 fusion.7
  39.5 1.3 copy.29
  40.8 0.4 copy.32
  41.3 1.4 copy.34
  42.7 0.4 fusion.4
  43.1 0.0 copy-start.4
  43.1 1.4 fusion.5
  44.5 0.0 copy-done
  44.5 0.0 copy-start.5
  44.5 7.0 %fusion.2.mid_ref = bf16[256,2048]{1,0:T(8,128)(2,1)} fusion(bf16[256,2048]{1,0:T(8,128)(2,1)S(1)} %copy-done, bf16[2048,2048]{1,0:T(8,128)(2,1)} %param.20, bf16[256,2048]{1,0:T(8,128)(2,1)} %param.15), kind=kOutput, calls=%fused_computation.4 | convolution fusion | flops 2150105088 | bytes 11534336 | tf_op jit(solution)/shard_map/dot_general | solution.py:242
  51.5 0.0 copy-done.5
  51.5 12.7 %convolution_convert_fusion = bf16[256,6144]{1,0:T(8,128)(2,1)} fusion(bf16[256,2048]{1,0:T(8,128)(2,1)S(1)} %copy-done.5, bf16[2048,6144]{1,0:T(8,128)(2,1)} %param.19), kind=kOutput, calls=%fused_computation | convolution fusion | flops 6444023808 | bytes 29360128 | tf_op jit(solution)/shard_map/dot_general | solution.py:251
  64.2 42.7 %all-gather.6.cloned.1.call-done = bf16[2048,2048]{1,0:T(8,128)(2,1)} async-done(((bf16[256,2048]{1,0:T(8,128)(2,1)}), bf16[2048,2048]{1,0:T(8,128)(2,1)}) %all-gather.6.cloned.1.call-update) | async-done | bytes 8388624 | tf_op jit(solution)/shard_map/all_gather | solution.py:233
  106.9 0.1 all-gather.8.cloned.1.call-update
  107.0 0.2 reduce-scatter.2.cloned.1.call-start
  107.2 0.0 copy-done.4
  107.2 0.9 copy.35.rank_ref
  108.2 0.0 collective-permute-done.refs_3_
  108.2 0.0 collective-permute-done.1.refs_4_
  108.2 0.0 collective-permute-done.2.refs_5_
  108.2 93.5 %shard_map.139 = f32[8,256,2048]{2,1,0:T(8,128)} custom-call(s32[8,8,256]{2,1,0:T(8,128)} %copy.35.rank_ref, s32[8,256,8]{2,1,0:T(8,128)} %bitcast.37, f32[8,256,8]{2,1,0:T(8,128)} %bitcast.36, bf16[8,256,2048]{2,1,0:T(8,128)(2,1)} %bitcast.39, bf16[4,2048,1024]{2,1,0:T(8,128)(2,1)} %refs_0_.3, bf16[4,2048,1024]{2,1,0:T(8,128)(2,1)} %refs_1_.3, ...), custom_call_target="tpu_custom_call" | custom-call | flops 68719476736 | bytes 167772160 | tf_op jit(solution)/shard_map/pallas_call | solution.py:103
  201.7 0.0 copy-start.3
  201.7 0.1 reduce-scatter.2.cloned.1.call-update
  201.7 1.2 copy-done.3
  202.9 0.9 copy.36.rank_ref
  203.8 0.0 all-gather.8.cloned.1.call-done
  203.8 93.4 %shard_map.140.part_ref = f32[8,256,2048]{2,1,0:T(8,128)} custom-call(s32[8,8,256]{2,1,0:T(8,128)} %copy.36.rank_ref, s32[8,256,8]{2,1,0:T(8,128)} %bitcast.35, f32[8,256,8]{2,1,0:T(8,128)} %bitcast.34, bf16[8,256,2048]{2,1,0:T(8,128)(2,1)} %bitcast.40, bf16[4,2048,1024]{2,1,0:T(8,128)(2,1)} %refs_0_.3, bf16[4,2048,1024]{2,1,0:T(8,128)(2,1)} %refs_1_.3, ...), custom_call_target="tpu_custom_call" | custom-call | flops 68719476736 | bytes 167772160 | tf_op jit(solution)/shard_map/pallas_call | solution.py:103
  297.3 0.0 copy-start.2
  297.3 0.0 copy-start.1
  297.3 230.8 %shard_map.141 = bf16[256,2048]{1,0:T(8,128)(2,1)} custom-call(f32[8,256,2048]{2,1,0:T(8,128)} %shard_map.140.part_ref, bf16[256,2048]{1,0:T(8,128)(2,1)} %fusion.2.mid_ref), custom_call_target="tpu_custom_call" | custom-call | flops 80000000000 | bytes 20971520 | tf_op jit(solution)/shard_map/pallas_call | solution.py:208
  528.1 0.0 reduce-scatter.2.cloned.1.call-done
  528.1 0.0 copy-done.2
  528.1 2.8 fusion.3
  530.9 2.3 copy.41
  533.2 0.0 copy-done.1
  (8 shorter events, 0.1 us)
Async XLA Ops:
  7.2 37.3 %copy-start = (bf16[256,2048]{1,0:T(8,128)(2,1)S(1)}, bf16[256,2048]{1,0:T(8,128)(2,1)}, u32[]{:S(2)}) copy-start(bf16[256,2048]{1,0:T(8,128)(2,1)} %param.16) | copy-start | bytes 3145732
  7.2 99.7 %all-gather.6.cloned.1.call-start = ((), (), s32[]{:S(2)}) async-start(), calls=%async_computation.2 | async-start | bytes 9437184 | tf_op jit(solution)/shard_map/all_gather | solution.py:233
  8.0 195.8 %all-gather.8.cloned.1.call-start = ((), (), s32[]{:S(2)}) async-start(), calls=%async_computation.3 | async-start | bytes 9437184 | tf_op jit(solution)/shard_map/all_gather | solution.py:233
  8.1 100.1 %collective-permute-start = (bf16[4,2048,1024]{2,1,0:T(8,128)(2,1)}, bf16[4,2048,1024]{2,1,0:T(8,128)(2,1)}, u32[]{:S(2)}, u32[]{:S(2)}) collective-permute-start(bf16[4,2048,1024]{2,1,0:T(8,128)(2,1)} %refs_0_.3), channel_id=1, source_target_pairs={{0,1},{1,0},{2,3},{3,2},{4,5},{5,4},{6,7},{7,6},{8,9},{9,8},{10,11... | collective-permute-start | bytes 50331656 | tf_op jit(solution)/shard_map/ppermute | solution.py:241
  12.8 95.4 %collective-permute-start.1 = (bf16[4,2048,1024]{2,1,0:T(8,128)(2,1)}, bf16[4,2048,1024]{2,1,0:T(8,128)(2,1)}, u32[]{:S(2)}, u32[]{:S(2)}) collective-permute-start(bf16[4,2048,1024]{2,1,0:T(8,128)(2,1)} %refs_1_.3), channel_id=1, source_target_pairs={{0,1},{1,0},{2,3},{3,2},{4,5},{5,4},{6,7},{7,6},{8,9},{9,8},{10,11... | collective-permute-start | bytes 50331656 | tf_op jit(solution)/shard_map/ppermute | solution.py:241
  13.0 95.2 %collective-permute-start.2 = (bf16[4,1024,2048]{2,1,0:T(8,128)(2,1)}, bf16[4,1024,2048]{2,1,0:T(8,128)(2,1)}, u32[]{:S(2)}, u32[]{:S(2)}) collective-permute-start(bf16[4,1024,2048]{2,1,0:T(8,128)(2,1)} %refs_2_.3), channel_id=1, source_target_pairs={{0,1},{1,0},{2,3},{3,2},{4,5},{5,4},{6,7},{7,6},{8,9},{9,8},{10,11... | collective-permute-start | bytes 50331656 | tf_op jit(solution)/shard_map/ppermute | solution.py:241
  43.1 64.2 %copy-start.4 = (s32[8,8,256]{1,2,0:T(8,128)}, s32[8,8,256]{1,2,0:T(8,128)S(1)}, u32[]{:S(2)}) copy-start(s32[8,8,256]{1,2,0:T(8,128)S(1)} %fusion.4) | copy-start | bytes 196612
  44.5 7.0 %copy-start.5 = (bf16[256,2048]{1,0:T(8,128)(2,1)S(1)}, bf16[256,2048]{1,0:T(8,128)(2,1)}, u32[]{:S(2)}) copy-start(bf16[256,2048]{1,0:T(8,128)(2,1)} %param.15) | copy-start | bytes 3145732
  107.0 421.1 %reduce-scatter.2.cloned.1.call-start = ((), (), s32[]{:S(2)}) async-start(), calls=%async_computation.1 | async-start | bytes 18874368 | tf_op jit(solution)/shard_map/reduce_scatter | solution.py:256
  201.7 1.2 copy-start.3
  297.3 230.8 %copy-start.2 = (bf16[256,2048]{1,0:T(8,128)(2,1)S(1)}, bf16[256,2048]{1,0:T(8,128)(2,1)}, u32[]{:S(2)}) copy-start(bf16[256,2048]{1,0:T(8,128)(2,1)} %param.12) | copy-start | bytes 3145732
  297.3 236.0 %copy-start.1 = (bf16[256,2048]{1,0:T(8,128)(2,1)S(1)}, bf16[256,2048]{1,0:T(8,128)(2,1)}, u32[]{:S(2)}) copy-start(bf16[256,2048]{1,0:T(8,128)(2,1)} %param.16) | copy-start | bytes 3145732
Sparse Core Ops, SparseCore 0:
  9.6 97.2 all-gather.5
  108.5 88.7 all-gather.7
  201.9 232.6 reduce-scatter.1

commit v3 on v2

--- a/solution.py
+++ b/solution.py
@@ -10,10 +10,8 @@
 CORES = 2
 
 
-def slot_tables(route_all, gate_all, expert_ids):
-    n_src, tok_n, top_k = route_all.shape
-    route_t = jnp.swapaxes(route_all, 1, 2)
-    gate_t = jnp.swapaxes(gate_all, 1, 2)
+def slot_tables(route_t, gate_t, expert_ids):
+    n_src, top_k, tok_n = route_t.shape
     hit = route_t[:, :, None, :] == expert_ids[None, None, :, None]
     chosen = jnp.any(hit, axis=1)
     gate = jnp.sum(jnp.where(hit, gate_t[:, :, None, :], 0.0), axis=1)
@@ -23,13 +21,14 @@
     return rank, jnp.swapaxes(rank, 1, 2), jnp.swapaxes(gate, 1, 2)
 
 
-def moe_kernel(n_src, local_n, capacity, rank_ref, rank_t_ref, gate_ref, x_ref, *refs):
+def moe_kernel(n_src, local_n, capacity, n_x, rank_ref, rank_t_ref, gate_ref, *refs):
+    x_refs, refs = refs[:n_x], refs[n_x:]
     own, peer = refs[0:3], refs[3:6]
     out_ref, rows_ref = refs[6], refs[7]
     bufs, sems = refs[8:11], refs[11]
     n_exp = CORES * local_n
     step = pl.program_id(0)
-    tok_n, model_dim = x_ref.shape[1:]
+    tok_n, model_dim = rank_ref.shape[2], x_refs[0].shape[2]
 
     def load(side, idx, slot):
         for k in range(3):
@@ -45,7 +44,8 @@
         slot_no = lax.broadcasted_iota(jnp.int32, (capacity, tok_n), 0)
         picks = [jnp.where(slot_no == rank_ref[0, e : e + 1, :], 1.0, 0.0) for e in range(n_exp)]
         place = jnp.concatenate(picks, axis=0).astype(jnp.bfloat16)
-        rows_ref[step] = jnp.dot(place, x_ref[0], preferred_element_type=jnp.float32).astype(jnp.bfloat16)
+        x = x_refs[0][0] if n_x == 1 else jnp.concatenate([x_ref[0] for x_ref in x_refs], axis=0)
+        rows_ref[step] = jnp.dot(place, x, preferred_element_type=jnp.float32).astype(jnp.bfloat16)
 
     @pl.when(jnp.logical_and(step >= n_src, step < n_src + n_exp))
     def _():
@@ -88,8 +88,9 @@
         out_ref[0] = total
 
 
-def expert_sums(rows_all, tables, own, peer):
-    n_src, tok_n, model_dim = rows_all.shape
+def expert_sums(rows, tables, own, peer):
+    n_src, _, model_dim = rows[0].shape
+    tok_n = sum(part.shape[1] for part in rows)
     local_n, _, ff_dim = own[0].shape
     n_exp = CORES * local_n
     rank, rank_t, gate = tables
@@ -101,15 +102,15 @@
     slots = n_exp * capacity
     flops = n_src * slots * model_dim * (6 * ff_dim + 2 * tok_n * 4)
     return pl.pallas_call(
-        functools.partial(moe_kernel, n_src, local_n, capacity),
+        functools.partial(moe_kernel, n_src, local_n, capacity, len(rows)),
         grid=(n_src + n_exp + n_src,),
         out_shape=jax.ShapeDtypeStruct((n_src, tok_n, model_dim), jnp.float32),
         in_specs=[
             pl.BlockSpec((1, n_exp, tok_n), first),
             pl.BlockSpec((1, tok_n, n_exp), last),
             pl.BlockSpec((1, tok_n, n_exp), last),
-            pl.BlockSpec((1, tok_n, model_dim), first),
         ]
+        + [pl.BlockSpec((1, part.shape[1], model_dim), first) for part in rows]
         + [any_spec] * 6,
         out_specs=pl.BlockSpec((1, tok_n, model_dim), last),
         scratch_shapes=[
@@ -123,7 +124,7 @@
             dimension_semantics=('arbitrary',), vmem_limit_bytes=62 * 1024 * 1024
         ),
         cost_estimate=pl.CostEstimate(flops=flops, bytes_accessed=160 * 2**20, transcendentals=0),
-    )(rank, rank_t, gate, rows_all, *own, *peer)
+    )(rank, rank_t, gate, *rows, *own, *peer)
 
 
 def ring_kernel(n_src, n_devs, part_ref, mid_ref, out_ref, local, slots, load_sems, send_sems, recv_sems):
@@ -224,6 +225,80 @@
     )(part, mid)
 
 
+def spread_kernel(n_src, n_devs, x_ref, meta_ref, rows_ref, info_ref, send_sems, recv_sems):
+    half = x_ref.shape[0] // 2
+    me = lax.axis_index('ep')
+    pos = lax.div(me, CORES)
+    to = {1: lax.rem(me + CORES, n_devs), -1: lax.rem(me + n_devs - CORES, n_devs)}
+
+    barrier = pltpu.get_barrier_semaphore()
+    for way in (1, -1):
+        pl.semaphore_signal(barrier, inc=1, device_id={'ep': to[way]}, device_id_type=pl.DeviceIdType.MESH)
+    pl.semaphore_wait(barrier, 2)
+
+    far = n_src // 2
+    near = n_src - 1 - far
+    cuts = [None, pl.ds(0, half), pl.ds(half, half)]
+    chains = []
+    for kind, longer in ((0, 1), (1, 1), (2, -1)):
+        for way in (1, -1):
+            chains.append((kind, way, far if way == longer else near))
+
+    def place(kind, chip):
+        return info_ref.at[chip] if kind == 0 else rows_ref.at[chip, cuts[kind]]
+
+    copies = {}
+
+    def send(c, hop, src):
+        kind, way, _ = chains[c]
+        chip = lax.rem(pos + n_src - way * (hop - 1), n_src)
+        at = c * far + hop - 1
+        copies[c, hop] = pltpu.make_async_remote_copy(
+            src_ref=place(kind, chip) if src is None else src,
+            dst_ref=place(kind, chip),
+            send_sem=send_sems.at[at],
+            recv_sem=recv_sems.at[at],
+            device_id={'ep': to[way]},
+            device_id_type=pl.DeviceIdType.MESH,
+        )
+        copies[c, hop].start()
+
+    for c, (kind, way, dist) in enumerate(chains):
+        send(c, 1, meta_ref if kind == 0 else x_ref.at[cuts[kind]])
+    rows_ref[pos] = x_ref[...]
+    info_ref[pos] = meta_ref[...]
+    for hop in range(1, far + 1):
+        for c, (kind, way, dist) in enumerate(chains):
+            if hop > dist:
+                continue
+            copies[c, hop].wait_recv()
+            if hop < dist:
+                send(c, hop + 1, None)
+    for copy in copies.values():
+        copy.wait_send()
+
+
+def spread(x, first_row, meta, n_devs):
+    n_src = n_devs // CORES
+    count, model_dim = x.shape[0] - first_row, x.shape[1]
+    n_sems = 6 * (n_src // 2)
+    vmem = pl.BlockSpec(memory_space=pltpu.VMEM)
+    return pl.pallas_call(
+        functools.partial(spread_kernel, n_src, n_devs),
+        out_shape=(
+            jax.ShapeDtypeStruct((n_src, count, model_dim), x.dtype),
+            jax.ShapeDtypeStruct((n_src, *meta.shape), meta.dtype),
+        ),
+        in_specs=[vmem, vmem],
+        out_specs=(vmem, vmem),
+        scratch_shapes=[pltpu.SemaphoreType.DMA((n_sems,)), pltpu.SemaphoreType.DMA((n_sems,))],
+        compiler_params=pltpu.CompilerParams(
+            collective_id=1, has_side_effects=True, vmem_limit_bytes=16 * 1024 * 1024
+        ),
+        cost_estimate=pl.CostEstimate(flops=30 * 10**9, bytes_accessed=4 * 2**20, transcendentals=0),
+    )(x[first_row:], meta)
+
+
 def solution(mesh):
     n_devs = mesh.shape['ep']
     groups = [list(range(c, n_devs, CORES)) for c in range(CORES)]
@@ -237,24 +312,28 @@
         local_n = w_gate.shape[0]
         me = lax.axis_index('ep')
         own = (w_gate, w_up, w_down)
-        rows_a = gather(x_a)
+        split = x_a.shape[0] * 3 // 4
+        rows_a = gather(x_a[:split])
         peer = tuple(lax.ppermute(w, 'ep', swap) for w in own)
+        meta = [route_a.astype(jnp.float32), gate_a, route_b.astype(jnp.float32), gate_b]
+        meta = jnp.concatenate([part.T for part in meta], axis=0)
+        rest_a, meta = spread(x_a, split, meta, n_devs)
         proj_b = jnp.dot(attn_b, w_o, preferred_element_type=jnp.float32).astype(jnp.bfloat16)
         mid_b = (h_b.astype(jnp.float32) + proj_b.astype(jnp.float32)).astype(jnp.bfloat16)
-        meta = jnp.concatenate([route_a.astype(jnp.float32), gate_a, route_b.astype(jnp.float32), gate_b], axis=1)
-        meta = gather(meta)
         ids = meta.astype(jnp.int32)
         local = jnp.arange(local_n)
         expert_ids = jnp.concatenate([me * local_n + local, (me ^ 1) * local_n + local])
-        tables_a = slot_tables(ids[:, :, :k], meta[:, :, k : 2 * k], expert_ids)
-        tables_b = slot_tables(ids[:, :, 2 * k : 3 * k], meta[:, :, 3 * k :], expert_ids)
-        qkv_b = jnp.dot(h_b, w_qkv, preferred_element_type=jnp.float32).astype(jnp.bfloat16)
-        early = (rows_a, mid_b, tables_a, tables_b, qkv_b)
-        rows_a, sent_b, tables_a, tables_b, qkv_b = lax.optimization_barrier(early)
+        tables_a = slot_tables(ids[:, :k], meta[:, k : 2 * k], expert_ids)
+        tables_b = slot_tables(ids[:, 2 * k : 3 * k], meta[:, 3 * k :], expert_ids)
+        early = (rows_a, mid_b, tables_a, tables_b)
+        rows_a, sent_b, tables_a, tables_b = lax.optimization_barrier(early)
         rows_b = gather(sent_b)
-        part_a = expert_sums(rows_a, tables_a, own, peer)
+        part_a = expert_sums((rows_a, rest_a), tables_a, own, peer)
         sum_a = lax.psum_scatter(part_a, 'ep', axis_index_groups=groups)
-        part_b = expert_sums(rows_b, tables_b, own, peer)
+        part_b = expert_sums((rows_b,), tables_b, own, peer)
+        part_b, after_b = lax.optimization_barrier((part_b, h_b))
+        qkv_b = jnp.dot(after_b, w_qkv, preferred_element_type=jnp.float32).astype(jnp.bfloat16)
+        part_b, qkv_b = lax.optimization_barrier((part_b, qkv_b))
         out_b = ring_sum(part_b, mid_b, n_devs)
         out_a = (x_a.astype(jnp.float32) + sum_a).astype(jnp.bfloat16)
         return out_a, out_b, qkv_b

time: 540 us -> 539 us (level)
  Pallas kernels: 418 us -> 454 us
  blocking collectives: 22.8 us -> 0 us
  waiting for transfers between devices: 43.5 us -> 24.7 us
    pallas_call x2 -> x3, Pallas kernels: 187 us -> 236 us  [the longest x2 187 us: expert_sums(): pl.pallas_call(functools.partial(moe_kernel, n_src, local_n, capacity, le...]
    all_gather x1 -> x0, blocking collectives: 22.8 us -> none  [gather(): return lax.all_gather(vals, 'ep', axis_index_groups=groups)]
    all_gather x2, waiting for transfers between devices: 42.7 us -> 24.5 us  [gather(): return lax.all_gather(vals, 'ep', axis_index_groups=groups)]
    pallas_call x1, Pallas kernels: 231 us -> 218 us  [ring_sum(): pl.pallas_call(functools.partial(ring_kernel, n_src, n_devs), out_shape=j...]
  transfers between devices with their start and end apart: 6 -> 6, of which waited for: 1 -> 1; matrix products, arithmetic and copies ran while one was open for 6% -> 6% of each run, Pallas kernels for 77% -> 84%
where the time goes in v3:
time: 539 us; the launch traced here: 538 us
  Pallas kernels  454 us (84%)
  waiting for transfers between devices  24.7 us (5%)
  matrix products  21.5 us (4%)
  between operations  13.9 us (3%)
  local copies, waits for them, and re-layouts  13.4 us (2%)
  starting transfers between devices  5.64 us (1%)
    pallas_call x1, Pallas kernels, ring_sum(): pl.pallas_call(functools.partial(ring_kernel, n_src, n_devs), out_shape=j...  218 us
    pallas_call x2, Pallas kernels, expert_sums(): pl.pallas_call(functools.partial(moe_kernel, n_src, local_n, capacity, le...  187 us
    pallas_call x1, Pallas kernels, spread(): pl.pallas_call(functools.partial(spread_kernel, n_src, n_devs), out_shape...  48.6 us
    all_gather x2, waiting for transfers between devices, gather(): return lax.all_gather(vals, 'ep', axis_index_groups=groups)  24.5 us
    dot_general x1, matrix products, local_step(): jnp.dot(after_b, w_qkv, preferred_element_type=jnp.float32)  12.7 us
  transfers between devices with their start and end apart: 6, of which 1 were waited for; matrix products, arithmetic and copies ran while one was open for 6% of the time, Pallas kernels for 84%

profile of v3, /device:TPU:21, one launch (start us, length us, event | category | flops | bytes accessed | tf_op | source)
XLA Modules:
  0.0 538.1 jit_solution(11902452857672553350)
XLA Ops:
  7.2 0.0 copy-start
  7.2 0.1 all-gather.5.cloned.1.call-start
  7.3 2.2 slice.18
  9.4 0.1 all-gather.5.cloned.1.call-update
  9.5 0.1 all-gather.7.cloned.1.call-start
  9.6 4.8 collective-permute-start
  14.3 0.1 collective-permute-start.1
  14.5 0.4 collective-permute-start.2
  14.8 1.0 slice.19.x_ref
  15.8 0.7 convert_bitcast_fusion
  16.5 0.7 pad_maximum_fusion.meta_ref
  17.2 48.6 %shard_map.139 = (bf16[8,64,2048]{2,1,0:T(8,128)(2,1)S(1)}, f32[8,32,256]{2,1,0:T(8,128)S(1)}) custom-call(bf16[64,2048]{1,0:T(8,128)(2,1)S(1)} %slice.19.x_ref, f32[32,256]{1,0:T(8,128)S(1)} %pad_maximum_fusion.meta_ref), custom_call_target="tpu_custom_call" | custom-call | flops 30000001024 | bytes 4194304 | tf_op jit(solution)/shard_map/pallas_call | solution.py:286
  65.8 0.0 copy-start.2
  65.8 1.3 copy-done.2
  67.2 0.1 pad_add_fusion
  67.3 0.2 compare_reduce_fusion
  67.5 0.4 copy.22
  68.0 0.2 fusion.7
  68.2 1.3 copy.23
  69.5 0.4 copy.25
  69.9 1.4 copy.26
  71.3 0.4 fusion.4
  71.7 0.0 copy-start.5
  71.7 1.4 fusion.5
  73.2 0.0 copy-done
  73.2 6.9 %fusion.2.mid_ref = bf16[256,2048]{1,0:T(8,128)(2,1)} fusion(bf16[256,2048]{1,0:T(8,128)(2,1)S(1)} %copy-done, bf16[2048,2048]{1,0:T(8,128)(2,1)} %param.20, bf16[256,2048]{1,0:T(8,128)(2,1)} %param.15), kind=kOutput, calls=%fused_computation.4 | convolution fusion | flops 2150105088 | bytes 11534336 | tf_op jit(solution)/shard_map/dot_general | solution.py:321
  80.1 24.5 %all-gather.5.cloned.1.call-done = bf16[1536,2048]{1,0:T(8,128)(2,1)} async-done(((bf16[192,2048]{1,0:T(8,128)(2,1)}), bf16[1536,2048]{1,0:T(8,128)(2,1)}) %all-gather.5.cloned.1.call-update) | async-done | bytes 6291472 | tf_op jit(solution)/shard_map/all_gather | solution.py:308
  104.5 0.1 all-gather.7.cloned.1.call-update
  104.6 0.2 reduce-scatter.2.cloned.1.call-start
  104.9 0.0 copy-done.5
  104.9 0.9 copy.27.rank_ref
  105.8 0.0 collective-permute-done.refs_5_.refs_4_
  105.8 0.0 collective-permute-done.1.refs_6_.refs_5_
  105.8 0.0 collective-permute-done.2.refs_7_.refs_6_
  105.8 93.6 %shard_map.140 = f32[8,256,2048]{2,1,0:T(8,128)} custom-call(s32[8,8,256]{2,1,0:T(8,128)} %copy.27.rank_ref, s32[8,256,8]{2,1,0:T(8,128)} %bitcast.29, f32[8,256,8]{2,1,0:T(8,128)} %bitcast.28, bf16[8,192,2048]{2,1,0:T(8,128)(2,1)} %bitcast.33, bf16[8,64,2048]{2,1,0:T(8,128)(2,1)} %copy-done.2, bf16[4,2048,1024]{2,1,0:T(8,128)(2,1)} %refs_1_.1, ...), custom_call_target="tpu_custom_call" | custom-call | flops 68719476736 | bytes 167772160 | tf_op jit(solution)/shard_map/pallas_call | solution.py:104
  199.4 0.0 copy-start.4
  199.4 0.1 reduce-scatter.2.cloned.1.call-update
  199.5 1.2 copy-done.4
  200.6 0.9 copy.28.rank_ref
  201.6 0.0 all-gather.7.cloned.1.call-done
  201.6 0.0 copy-start.6
  201.6 93.7 %shard_map.141.part_ref = f32[8,256,2048]{2,1,0:T(8,128)} custom-call(s32[8,8,256]{2,1,0:T(8,128)} %copy.28.rank_ref, s32[8,256,8]{2,1,0:T(8,128)} %bitcast.27, f32[8,256,8]{2,1,0:T(8,128)} %bitcast.26, bf16[8,256,2048]{2,1,0:T(8,128)(2,1)} %bitcast.32, bf16[4,2048,1024]{2,1,0:T(8,128)(2,1)} %refs_1_.1, bf16[4,2048,1024]{2,1,0:T(8,128)(2,1)} %refs_2_.3, ...), custom_call_target="tpu_custom_call" | custom-call | flops 68719476736 | bytes 167772160 | tf_op jit(solution)/shard_map/pallas_call | solution.py:104
  295.3 0.0 copy-done.6
  295.3 12.7 %convolution_convert_fusion = bf16[256,6144]{1,0:T(8,128)(2,1)} fusion(bf16[256,2048]{1,0:T(8,128)(2,1)S(1)} %copy-done.6, bf16[2048,6144]{1,0:T(8,128)(2,1)} %param.19), kind=kOutput, calls=%fused_computation | convolution fusion | flops 6444023808 | bytes 29360128 | tf_op jit(solution)/shard_map/dot_general | solution.py:335
  308.0 0.0 copy-start.3
  308.0 0.0 copy-start.1
  308.0 218.4 %shard_map.142 = bf16[256,2048]{1,0:T(8,128)(2,1)} custom-call(f32[8,256,2048]{2,1,0:T(8,128)} %shard_map.141.part_ref, bf16[256,2048]{1,0:T(8,128)(2,1)} %fusion.2.mid_ref), custom_call_target="tpu_custom_call" | custom-call | flops 80000000000 | bytes 20971520 | tf_op jit(solution)/shard_map/pallas_call | solution.py:209
  526.4 0.0 reduce-scatter.2.cloned.1.call-done
  526.4 0.0 copy-done.3
  526.4 2.8 fusion.3
  529.3 2.3 copy.32
  531.6 0.0 copy-done.1
  (4 shorter events, 0.0 us)
Async XLA Ops:
  7.2 66.0 %copy-start = (bf16[256,2048]{1,0:T(8,128)(2,1)S(1)}, bf16[256,2048]{1,0:T(8,128)(2,1)}, u32[]{:S(2)}) copy-start(bf16[256,2048]{1,0:T(8,128)(2,1)} %param.16) | copy-start | bytes 3145732
  7.2 97.4 %all-gather.5.cloned.1.call-start = ((), (), s32[]{:S(2)}) async-start(), calls=%async_computation.2 | async-start | bytes 7077888 | tf_op jit(solution)/shard_map/all_gather | solution.py:308
  9.5 192.1 %all-gather.7.cloned.1.call-start = ((), (), s32[]{:S(2)}) async-start(), calls=%async_computation.3 | async-start | bytes 9437184 | tf_op jit(solution)/shard_map/all_gather | solution.py:308
  9.6 96.2 %collective-permute-start = (bf16[4,2048,1024]{2,1,0:T(8,128)(2,1)}, bf16[4,2048,1024]{2,1,0:T(8,128)(2,1)}, u32[]{:S(2)}, u32[]{:S(2)}) collective-permute-start(bf16[4,2048,1024]{2,1,0:T(8,128)(2,1)} %refs_1_.1), channel_id=1, source_target_pairs={{0,1},{1,0},{2,3},{3,2},{4,5},{5,4},{6,7},{7,6},{8,9},{9,8},{10,11... | collective-permute-start | bytes 50331656 | tf_op jit(solution)/shard_map/ppermute | solution.py:317
  14.3 91.5 %collective-permute-start.1 = (bf16[4,2048,1024]{2,1,0:T(8,128)(2,1)}, bf16[4,2048,1024]{2,1,0:T(8,128)(2,1)}, u32[]{:S(2)}, u32[]{:S(2)}) collective-permute-start(bf16[4,2048,1024]{2,1,0:T(8,128)(2,1)} %refs_2_.3), channel_id=1, source_target_pairs={{0,1},{1,0},{2,3},{3,2},{4,5},{5,4},{6,7},{7,6},{8,9},{9,8},{10,11... | collective-permute-start | bytes 50331656 | tf_op jit(solution)/shard_map/ppermute | solution.py:317
  14.5 91.3 %collective-permute-start.2 = (bf16[4,1024,2048]{2,1,0:T(8,128)(2,1)}, bf16[4,1024,2048]{2,1,0:T(8,128)(2,1)}, u32[]{:S(2)}, u32[]{:S(2)}) collective-permute-start(bf16[4,1024,2048]{2,1,0:T(8,128)(2,1)} %refs_3_.3), channel_id=1, source_target_pairs={{0,1},{1,0},{2,3},{3,2},{4,5},{5,4},{6,7},{7,6},{8,9},{9,8},{10,11... | collective-permute-start | bytes 50331656 | tf_op jit(solution)/shard_map/ppermute | solution.py:317
  65.8 1.3 copy-start.2
  71.7 33.1 %copy-start.5 = (s32[8,8,256]{1,2,0:T(8,128)}, s32[8,8,256]{1,2,0:T(8,128)S(1)}, u32[]{:S(2)}) copy-start(s32[8,8,256]{1,2,0:T(8,128)S(1)} %fusion.4) | copy-start | bytes 196612
  104.6 421.8 %reduce-scatter.2.cloned.1.call-start = ((), (), s32[]{:S(2)}) async-start(), calls=%async_computation.1 | async-start | bytes 18874368 | tf_op jit(solution)/shard_map/reduce_scatter | solution.py:332
  199.4 1.2 copy-start.4
  201.6 93.7 %copy-start.6 = (bf16[256,2048]{1,0:T(8,128)(2,1)S(1)}, bf16[256,2048]{1,0:T(8,128)(2,1)}, u32[]{:S(2)}) copy-start(bf16[256,2048]{1,0:T(8,128)(2,1)} %param.15) | copy-start | bytes 3145732
  308.0 218.4 %copy-start.3 = (bf16[256,2048]{1,0:T(8,128)(2,1)S(1)}, bf16[256,2048]{1,0:T(8,128)(2,1)}, u32[]{:S(2)}) copy-start(bf16[256,2048]{1,0:T(8,128)(2,1)} %param.12) | copy-start | bytes 3145732
  308.0 223.6 %copy-start.1 = (bf16[256,2048]{1,0:T(8,128)(2,1)S(1)}, bf16[256,2048]{1,0:T(8,128)(2,1)}, u32[]{:S(2)}) copy-start(bf16[256,2048]{1,0:T(8,128)(2,1)} %param.16) | copy-start | bytes 3145732
Sparse Core Ops, SparseCore 0:
  9.6 94.8 all-gather.4
  106.1 89.3 all-gather.6
  199.6 220.8 reduce-scatter.1

commit v4 on v3

--- a/solution.py
+++ b/solution.py
@@ -325,15 +325,13 @@
         expert_ids = jnp.concatenate([me * local_n + local, (me ^ 1) * local_n + local])
         tables_a = slot_tables(ids[:, :k], meta[:, k : 2 * k], expert_ids)
         tables_b = slot_tables(ids[:, 2 * k : 3 * k], meta[:, 3 * k :], expert_ids)
-        early = (rows_a, mid_b, tables_a, tables_b)
-        rows_a, sent_b, tables_a, tables_b = lax.optimization_barrier(early)
+        qkv_b = jnp.dot(h_b, w_qkv, preferred_element_type=jnp.float32).astype(jnp.bfloat16)
+        early = (rows_a, mid_b, tables_a, tables_b, qkv_b)
+        rows_a, sent_b, tables_a, tables_b, qkv_b = lax.optimization_barrier(early)
         rows_b = gather(sent_b)
         part_a = expert_sums((rows_a, rest_a), tables_a, own, peer)
         sum_a = lax.psum_scatter(part_a, 'ep', axis_index_groups=groups)
         part_b = expert_sums((rows_b,), tables_b, own, peer)
-        part_b, after_b = lax.optimization_barrier((part_b, h_b))
-        qkv_b = jnp.dot(after_b, w_qkv, preferred_element_type=jnp.float32).astype(jnp.bfloat16)
-        part_b, qkv_b = lax.optimization_barrier((part_b, qkv_b))
         out_b = ring_sum(part_b, mid_b, n_devs)
         out_a = (x_a.astype(jnp.float32) + sum_a).astype(jnp.bfloat16)
         return out_a, out_b, qkv_b

time: 539 us -> 539 us (level)
  Pallas kernels: 454 us -> 467 us
  waiting for transfers between devices: 24.7 us -> 11.8 us
    pallas_call x1, Pallas kernels: 218 us -> 231 us  [ring_sum(): pl.pallas_call(functools.partial(ring_kernel, n_src, n_devs), out_shape=j...]
    all_gather x2, waiting for transfers between devices: 24.5 us -> 11.7 us  [gather(): return lax.all_gather(vals, 'ep', axis_index_groups=groups)]
  transfers between devices with their start and end apart: 6 -> 6, of which waited for: 1 -> 1; matrix products, arithmetic and copies ran while one was open for 6% -> 6% of each run, Pallas kernels for 84% -> 87%
where the time goes in v4:
time: 539 us; the launch traced here: 538 us
  Pallas kernels  467 us (87%)
  matrix products  21.5 us (4%)
  between operations  13.9 us (3%)
  local copies, waits for them, and re-layouts  13.4 us (2%)
  waiting for transfers between devices  11.8 us (2%)
  starting transfers between devices  5.64 us (1%)
    pallas_call x1, Pallas kernels, ring_sum(): pl.pallas_call(functools.partial(ring_kernel, n_src, n_devs), out_shape=j...  231 us
    pallas_call x2, Pallas kernels, expert_sums(): pl.pallas_call(functools.partial(moe_kernel, n_src, local_n, capacity, le...  187 us
    pallas_call x1, Pallas kernels, spread(): pl.pallas_call(functools.partial(spread_kernel, n_src, n_devs), out_shape...  48.6 us
    dot_general x1, matrix products, local_step(): jnp.dot(h_b, w_qkv, preferred_element_type=jnp.float32).astype(jnp.bfloat16)  12.7 us
    all_gather x2, waiting for transfers between devices, gather(): return lax.all_gather(vals, 'ep', axis_index_groups=groups)  11.7 us
  transfers between devices with their start and end apart: 6, of which 1 were waited for; matrix products, arithmetic and copies ran while one was open for 6% of the time, Pallas kernels for 87%

profile of v4, /device:TPU:21, one launch (start us, length us, event | category | flops | bytes accessed | tf_op | source)
XLA Modules:
  0.0 538.1 jit_solution(8906636098373225035)
XLA Ops:
  7.2 0.0 copy-start
  7.2 0.1 all-gather.5.cloned.1.call-start
  7.3 2.2 slice.18
  9.4 0.1 all-gather.5.cloned.1.call-update
  9.5 0.1 all-gather.7.cloned.1.call-start
  9.6 4.8 collective-permute-start
  14.3 0.1 collective-permute-start.1
  14.5 0.4 collective-permute-start.2
  14.8 1.0 slice.19.x_ref
  15.8 0.7 convert_bitcast_fusion
  16.5 0.7 pad_maximum_fusion.meta_ref
  17.2 48.6 %shard_map.139 = (bf16[8,64,2048]{2,1,0:T(8,128)(2,1)S(1)}, f32[8,32,256]{2,1,0:T(8,128)S(1)}) custom-call(bf16[64,2048]{1,0:T(8,128)(2,1)S(1)} %slice.19.x_ref, f32[32,256]{1,0:T(8,128)S(1)} %pad_maximum_fusion.meta_ref), custom_call_target="tpu_custom_call" | custom-call | flops 30000001024 | bytes 4194304 | tf_op jit(solution)/shard_map/pallas_call | solution.py:286
  65.8 0.0 copy-start.2
  65.8 1.3 copy-done.2
  67.2 0.1 pad_add_fusion
  67.3 0.2 compare_reduce_fusion
  67.5 0.4 copy.22
  68.0 0.2 fusion.7
  68.2 1.3 copy.23
  69.5 0.4 copy.25
  69.9 1.4 copy.26
  71.3 0.4 fusion.4
  71.7 0.0 copy-start.5
  71.7 1.4 fusion.5
  73.2 0.0 copy-done
  73.2 0.0 copy-start.6
  73.2 7.0 %fusion.2.mid_ref = bf16[256,2048]{1,0:T(8,128)(2,1)} fusion(bf16[256,2048]{1,0:T(8,128)(2,1)S(1)} %copy-done, bf16[2048,2048]{1,0:T(8,128)(2,1)} %param.20, bf16[256,2048]{1,0:T(8,128)(2,1)} %param.15), kind=kOutput, calls=%fused_computation.4 | convolution fusion | flops 2150105088 | bytes 11534336 | tf_op jit(solution)/shard_map/dot_general | solution.py:321
  80.2 0.0 copy-done.6
  80.2 12.7 %convolution_convert_fusion = bf16[256,6144]{1,0:T(8,128)(2,1)} fusion(bf16[256,2048]{1,0:T(8,128)(2,1)S(1)} %copy-done.6, bf16[2048,6144]{1,0:T(8,128)(2,1)} %param.19), kind=kOutput, calls=%fused_computation | convolution fusion | flops 6444023808 | bytes 29360128 | tf_op jit(solution)/shard_map/dot_general | solution.py:328
  92.9 11.6 %all-gather.5.cloned.1.call-done = bf16[1536,2048]{1,0:T(8,128)(2,1)} async-done(((bf16[192,2048]{1,0:T(8,128)(2,1)}), bf16[1536,2048]{1,0:T(8,128)(2,1)}) %all-gather.5.cloned.1.call-update) | async-done | bytes 6291472 | tf_op jit(solution)/shard_map/all_gather | solution.py:308
  104.5 0.1 all-gather.7.cloned.1.call-update
  104.6 0.2 reduce-scatter.2.cloned.1.call-start
  104.9 0.0 copy-done.5
  104.9 0.9 copy.27.rank_ref
  105.8 0.0 collective-permute-done.refs_5_.refs_4_
  105.8 0.0 collective-permute-done.1.refs_6_.refs_5_
  105.8 0.0 collective-permute-done.2.refs_7_.refs_6_
  105.8 93.6 %shard_map.140 = f32[8,256,2048]{2,1,0:T(8,128)} custom-call(s32[8,8,256]{2,1,0:T(8,128)} %copy.27.rank_ref, s32[8,256,8]{2,1,0:T(8,128)} %bitcast.29, f32[8,256,8]{2,1,0:T(8,128)} %bitcast.28, bf16[8,192,2048]{2,1,0:T(8,128)(2,1)} %bitcast.33, bf16[8,64,2048]{2,1,0:T(8,128)(2,1)} %copy-done.2, bf16[4,2048,1024]{2,1,0:T(8,128)(2,1)} %refs_1_.1, ...), custom_call_target="tpu_custom_call" | custom-call | flops 68719476736 | bytes 167772160 | tf_op jit(solution)/shard_map/pallas_call | solution.py:104
  199.4 0.0 copy-start.4
  199.4 0.1 reduce-scatter.2.cloned.1.call-update
  199.5 1.2 copy-done.4
  200.6 0.9 copy.28.rank_ref
  201.6 0.0 all-gather.7.cloned.1.call-done
  201.6 93.4 %shard_map.141.part_ref = f32[8,256,2048]{2,1,0:T(8,128)} custom-call(s32[8,8,256]{2,1,0:T(8,128)} %copy.28.rank_ref, s32[8,256,8]{2,1,0:T(8,128)} %bitcast.27, f32[8,256,8]{2,1,0:T(8,128)} %bitcast.26, bf16[8,256,2048]{2,1,0:T(8,128)(2,1)} %bitcast.32, bf16[4,2048,1024]{2,1,0:T(8,128)(2,1)} %refs_1_.1, bf16[4,2048,1024]{2,1,0:T(8,128)(2,1)} %refs_2_.3, ...), custom_call_target="tpu_custom_call" | custom-call | flops 68719476736 | bytes 167772160 | tf_op jit(solution)/shard_map/pallas_call | solution.py:104
  295.0 0.0 copy-start.3
  295.0 0.0 copy-start.1
  295.0 231.4 %shard_map.142 = bf16[256,2048]{1,0:T(8,128)(2,1)} custom-call(f32[8,256,2048]{2,1,0:T(8,128)} %shard_map.141.part_ref, bf16[256,2048]{1,0:T(8,128)(2,1)} %fusion.2.mid_ref), custom_call_target="tpu_custom_call" | custom-call | flops 80000000000 | bytes 20971520 | tf_op jit(solution)/shard_map/pallas_call | solution.py:209
  526.4 0.0 reduce-scatter.2.cloned.1.call-done
  526.4 0.0 copy-done.3
  526.5 2.8 fusion.3
  529.3 2.3 copy.32
  531.6 0.0 copy-done.1
  (4 shorter events, 0.0 us)
Async XLA Ops:
  7.2 66.0 %copy-start = (bf16[256,2048]{1,0:T(8,128)(2,1)S(1)}, bf16[256,2048]{1,0:T(8,128)(2,1)}, u32[]{:S(2)}) copy-start(bf16[256,2048]{1,0:T(8,128)(2,1)} %param.16) | copy-start | bytes 3145732
  7.2 97.4 %all-gather.5.cloned.1.call-start = ((), (), s32[]{:S(2)}) async-start(), calls=%async_computation.2 | async-start | bytes 7077888 | tf_op jit(solution)/shard_map/all_gather | solution.py:308
  9.5 192.1 %all-gather.7.cloned.1.call-start = ((), (), s32[]{:S(2)}) async-start(), calls=%async_computation.3 | async-start | bytes 9437184 | tf_op jit(solution)/shard_map/all_gather | solution.py:308
  9.6 96.2 %collective-permute-start = (bf16[4,2048,1024]{2,1,0:T(8,128)(2,1)}, bf16[4,2048,1024]{2,1,0:T(8,128)(2,1)}, u32[]{:S(2)}, u32[]{:S(2)}) collective-permute-start(bf16[4,2048,1024]{2,1,0:T(8,128)(2,1)} %refs_1_.1), channel_id=1, source_target_pairs={{0,1},{1,0},{2,3},{3,2},{4,5},{5,4},{6,7},{7,6},{8,9},{9,8},{10,11... | collective-permute-start | bytes 50331656 | tf_op jit(solution)/shard_map/ppermute | solution.py:317
  14.3 91.5 %collective-permute-start.1 = (bf16[4,2048,1024]{2,1,0:T(8,128)(2,1)}, bf16[4,2048,1024]{2,1,0:T(8,128)(2,1)}, u32[]{:S(2)}, u32[]{:S(2)}) collective-permute-start(bf16[4,2048,1024]{2,1,0:T(8,128)(2,1)} %refs_2_.3), channel_id=1, source_target_pairs={{0,1},{1,0},{2,3},{3,2},{4,5},{5,4},{6,7},{7,6},{8,9},{9,8},{10,11... | collective-permute-start | bytes 50331656 | tf_op jit(solution)/shard_map/ppermute | solution.py:317
  14.5 91.3 %collective-permute-start.2 = (bf16[4,1024,2048]{2,1,0:T(8,128)(2,1)}, bf16[4,1024,2048]{2,1,0:T(8,128)(2,1)}, u32[]{:S(2)}, u32[]{:S(2)}) collective-permute-start(bf16[4,1024,2048]{2,1,0:T(8,128)(2,1)} %refs_3_.3), channel_id=1, source_target_pairs={{0,1},{1,0},{2,3},{3,2},{4,5},{5,4},{6,7},{7,6},{8,9},{9,8},{10,11... | collective-permute-start | bytes 50331656 | tf_op jit(solution)/shard_map/ppermute | solution.py:317
  65.8 1.3 copy-start.2
  71.7 33.1 %copy-start.5 = (s32[8,8,256]{1,2,0:T(8,128)}, s32[8,8,256]{1,2,0:T(8,128)S(1)}, u32[]{:S(2)}) copy-start(s32[8,8,256]{1,2,0:T(8,128)S(1)} %fusion.4) | copy-start | bytes 196612
  73.2 7.0 %copy-start.6 = (bf16[256,2048]{1,0:T(8,128)(2,1)S(1)}, bf16[256,2048]{1,0:T(8,128)(2,1)}, u32[]{:S(2)}) copy-start(bf16[256,2048]{1,0:T(8,128)(2,1)} %param.15) | copy-start | bytes 3145732
  104.6 421.8 %reduce-scatter.2.cloned.1.call-start = ((), (), s32[]{:S(2)}) async-start(), calls=%async_computation.1 | async-start | bytes 18874368 | tf_op jit(solution)/shard_map/reduce_scatter | solution.py:333
  199.4 1.2 copy-start.4
  295.0 231.4 %copy-start.3 = (bf16[256,2048]{1,0:T(8,128)(2,1)S(1)}, bf16[256,2048]{1,0:T(8,128)(2,1)}, u32[]{:S(2)}) copy-start(bf16[256,2048]{1,0:T(8,128)(2,1)} %param.12) | copy-start | bytes 3145732
  295.0 236.6 %copy-start.1 = (bf16[256,2048]{1,0:T(8,128)(2,1)S(1)}, bf16[256,2048]{1,0:T(8,128)(2,1)}, u32[]{:S(2)}) copy-start(bf16[256,2048]{1,0:T(8,128)(2,1)} %param.16) | copy-start | bytes 3145732
Sparse Core Ops, SparseCore 0:
  9.6 94.8 all-gather.4
  106.1 89.3 all-gather.6
  199.6 233.8 reduce-scatter.1
